TPU v7x, 256 devices: a whole 4x4x8 slice. The times are simulated.
256 devices in a mesh: dom: 32 (over y, z), sub: 8 (over x, core).
Axes of the slice: x: 4, y: 4, z: 8, core: 2. Of those that a mesh axis runs over, the one named last changes fastest.
Arguments:
- positions: float32 [16384, 3, 256], P(('dom', 'sub')), may hold values from -6 to 6
- time_bins: int32 [16384, 256], P(('dom', 'sub')), may hold values from 0 to 5
- home_groups: int32 [16384], P(('dom', 'sub')), may hold values from 0 to 63
- targets: int32 [16384, 4], P(('dom', 'sub')), may hold values from -1 to 31, as said below
- target_groups: int32 [16384, 4], P(('dom', 'sub')), may hold values from 0 to 63
- node_pos: float32 [3, 1048576], P(None, ('dom', 'sub')), may hold values from -6 to 6
- node_mass: float32 [1048576], P(('dom', 'sub')), may hold values from 0.2 to 2
- node_lists: int32 [2048, 256], P('dom'), may hold values from 0 to 32767
- list_counts: int32 [2048], P('dom'), may hold values from 64 to 256, as said below
Outputs:
- forces: float32 [16384, 3, 256], P(('dom', 'sub'))
Inputs may be any that keep to these rules, and one draw needn't show every extreme that they name: `targets`: row b names the remote domains that block b visits, each at most once and never its own domain b // 512; -1 marks an unused entry, in any column. The rows of one device name one domain at most 8 times, and some device names some domain exactly 8 times in every draw. The rows of one domain's 8 devices together name one domain at most 16 times, and this is reached in every draw. `list_counts`: each domain has at least one list with all 256 entries valid.
All inputs are finite; a program needn't handle non-finite values.
Results may differ from a plain program's by a relative error of at most 0.0003.
Values sent between devices are 32-bit elements; how exact they have to be, the bound alone decides.
A program may use at most 128 MiB of HBM per device.

v0:
```python
import jax
import jax.numpy as jnp
from jax import lax
from jax.sharding import PartitionSpec as P

CUR_BIN = 2


soften_sq = 0.04
gauss_slope = 1.1283791670955126


def sent_to_all(value, axis):
    length = lax.axis_size(axis)
    return lax.all_to_all(
        jnp.broadcast_to(value[None], (length, *value.shape)), axis, 0, 0, tiled=True
    )


def laid_out(blocks, dim):
    shape = list(blocks.shape[1:])
    shape[dim] *= blocks.shape[0]
    return jnp.moveaxis(blocks, 0, dim).reshape(shape)


def gathered_copies(value, axis, dim):
    blocks = sent_to_all(value, axis)
    return laid_out(blocks, dim)


def joined_by_halves(pieces, combine):
    while len(jax.tree.leaves(pieces)[0]) > 1:
        pieces = jax.vmap(combine)(*(pieces[side::2] for side in (0, 1)))
    return pieces[0]


def carried_in(value, axis, combine, identity):
    length, mine = (lax.axis_size(axis), lax.axis_index(axis))
    passed = jnp.arange(length) < mine

    def kept(part, zero, own):
        part = jnp.where(
            passed.reshape(-1, *(1 for _ in own.shape)), part, jnp.asarray(zero, own.dtype)
        )
        return part

    pieces = sent_to_all(value, axis)
    return joined_by_halves(kept(pieces, identity, value), combine)


def grouped_exchange(value, axis, split_dim, concat_dim, work, item_dim, out_dim):

    def moved(group):
        return lax.all_to_all(group, axis, split_axis=split_dim, concat_axis=concat_dim, tiled=True)

    items = jax.tree.leaves(value)[0].shape[item_dim]
    ends = [items * k // 2 for k in range(2 + 1)] if items % 2 == 0 else [0, items]
    groups = [
        jax.tree.map(lambda a: lax.slice_in_dim(a, low, high, axis=item_dim), value)
        for low, high in zip(ends, ends[1:])
    ]
    arrived = [moved(group) for group in groups]
    made = [work(group) for group in arrived]
    return jax.tree.map(lambda *parts: jnp.concatenate(parts, axis=out_dim), *made)


def short_pull(sink_pos, source_pos, source_mass):
    offset = sink_pos[:, None, :] - source_pos[:, :, None]
    range_sq = jnp.sum(offset * offset, axis=0) + soften_sq
    distance = jnp.sqrt(range_sq)
    scaled = distance * 0.5
    factor = lax.erfc(scaled) + gauss_slope * scaled * jnp.exp(-scaled * scaled)
    weight = source_mass[:, None] * factor / (range_sq * distance)
    return -jnp.sum(offset * weight[None, :, :], axis=1)


def list_tables(table_pos, table_mass, lists, counts):
    entry_ids = jnp.arange(lists.shape[1], dtype=jnp.int32)
    list_pos = jnp.transpose(table_pos[:, lists], (1, 0, 2))
    list_mass = table_mass[lists] * (entry_ids[None, :] < counts[:, None]).astype(jnp.float32)
    return (list_pos, list_mass)


def evaluate(sink_pos, list_rows, is_alive, list_pos, list_mass):
    item_count = sink_pos.shape[0]
    padded = -(-item_count // 8) * 8
    padding = padded - item_count
    if padding:
        sink_pos = jnp.concatenate(
            [sink_pos, jnp.zeros((padding,) + sink_pos.shape[1:], sink_pos.dtype)]
        )
        list_rows = jnp.concatenate([list_rows, jnp.zeros((padding,), jnp.int32)])
        is_alive = jnp.concatenate([is_alive, jnp.zeros((padding,), jnp.float32)])

    def one_item(sink_one, list_row, alive_one):
        return short_pull(sink_one, list_pos[list_row], list_mass[list_row] * alive_one)

    def one_group(operands):
        return jax.vmap(one_item)(*operands)

    width = sink_pos.shape[2]
    grouped = lax.map(
        one_group,
        (
            sink_pos.reshape(padded // 8, 8, 3, width),
            list_rows.reshape(padded // 8, 8),
            is_alive.reshape(padded // 8, 8),
        ),
    )
    return grouped.reshape(padded, 3, width)[:item_count]


def ranks_within(bucket, usable, bucket_count):
    onehot = (
        (bucket[:, None] == jnp.arange(bucket_count, dtype=jnp.int32)[None, :]) & usable[:, None]
    ).astype(jnp.int32)
    placed = jnp.sum((jnp.cumsum(onehot, axis=0) - onehot) * onehot, axis=1)
    return (placed, jnp.sum(onehot, axis=0))


def owners(slot_index, usable, slot_count):
    matches = (slot_index[None, :] == jnp.arange(slot_count, dtype=jnp.int32)[:, None]) & usable[
        None, :
    ]
    is_filled = jnp.any(matches, axis=1)
    source_row = jnp.sum(
        matches.astype(jnp.int32) * jnp.arange(slot_index.shape[0], dtype=jnp.int32)[None, :],
        axis=1,
    )
    return (source_row, is_filled)


def local(
    positions,
    time_bins,
    home_groups,
    targets,
    target_groups,
    node_pos,
    node_mass,
    node_lists,
    list_counts,
):
    domains = lax.axis_size("dom")
    sharers = lax.axis_size("sub")
    blocks, most_visits = targets.shape
    width = positions.shape[2]
    capacity = max(2, blocks * most_visits // domains)
    table_pos, table_mass = (
        gathered_copies(node_pos, "sub", 1),
        gathered_copies(node_mass, "sub", 0),
    )
    list_pos, list_mass = list_tables(table_pos, table_mass, node_lists, list_counts)
    home_force = evaluate(
        positions, home_groups, jnp.ones((blocks,), jnp.float32), list_pos, list_mass
    )

    def imported(arrived):
        arrived_pos, arrived_group = arrived
        leading = arrived_group.shape
        flat_group = arrived_group.reshape(-1)
        pulled = evaluate(
            arrived_pos.reshape((-1, 3, width)),
            jnp.maximum(flat_group, 0),
            (flat_group >= 0).astype(jnp.float32),
            list_pos,
            list_mass,
        )
        return pulled.reshape(leading + (3, width))

    flat_dest = targets.reshape(-1)
    usable = flat_dest >= 0
    safe_dest = jnp.maximum(flat_dest, 0)
    pair_block = jnp.arange(blocks * most_visits, dtype=jnp.int32) // most_visits
    flat_groups = target_groups.reshape(-1)
    within, per_domain = ranks_within(safe_dest, usable, domains)
    first_width = -(-capacity // sharers)
    second_width = -(-2 * capacity // sharers)
    offsets = carried_in(
        per_domain, "sub", lambda earlier, later: earlier + later, jnp.zeros_like(per_domain)
    )
    row_place = offsets[safe_dest] + within
    sharer_of = row_place % sharers
    row_slot = row_place // sharers
    bucket = sharer_of * domains + safe_dest
    within_bucket, _ = ranks_within(bucket, usable, sharers * domains)
    first_slot = bucket * first_width + within_bucket
    source_row, is_filled = owners(first_slot, usable, sharers * domains * first_width)
    out_pos = jnp.where(is_filled[:, None, None], positions[pair_block[source_row]], 0.0).reshape(
        sharers, domains, first_width, 3, width
    )
    out_group = jnp.where(is_filled, flat_groups[source_row], -1).reshape(
        sharers, domains, first_width
    )
    out_slot = jnp.where(is_filled, row_slot[source_row], 0).reshape(sharers, domains, first_width)
    spread_pos, spread_group, spread_slot = (
        lax.all_to_all(out_pos, "sub", split_axis=0, concat_axis=0, tiled=True),
        lax.all_to_all(out_group, "sub", split_axis=0, concat_axis=0, tiled=True),
        lax.all_to_all(out_slot, "sub", split_axis=0, concat_axis=0, tiled=True),
    )
    arrival_dest = (
        jnp.arange(sharers * domains * first_width, dtype=jnp.int32) // first_width % domains
    )
    arrival_group = spread_group.reshape(-1)
    arrival_ok = arrival_group >= 0
    second_index = arrival_dest * second_width + spread_slot.reshape(-1)
    arrival_row, second_filled = owners(second_index, arrival_ok, domains * second_width)
    mid_pos = jnp.where(
        second_filled[:, None, None], spread_pos.reshape(-1, 3, width)[arrival_row], 0.0
    ).reshape(domains, second_width, 3, width)
    mid_group = jnp.where(second_filled, arrival_group[arrival_row], -1).reshape(
        domains, second_width
    )
    computed = grouped_exchange((mid_pos, mid_group), "dom", 0, 0, imported, 1, 1)
    returned = lax.all_to_all(computed, "dom", split_axis=0, concat_axis=0, tiled=True)
    arrival_force = returned.reshape(domains * second_width, 3, width)[
        jnp.where(arrival_ok, second_index, 0)
    ]
    arrival_force = arrival_force * arrival_ok.astype(jnp.float32)[:, None, None]
    gathered_back = lax.all_to_all(
        arrival_force.reshape(sharers, domains, first_width, 3, width),
        "sub",
        split_axis=0,
        concat_axis=0,
        tiled=True,
    )
    pair_force = gathered_back.reshape(-1, 3, width)[jnp.where(usable, first_slot, 0)]
    pair_force = pair_force * usable.astype(jnp.float32)[:, None, None]
    remote = jnp.sum(pair_force.reshape(blocks, most_visits, 3, width), axis=1)
    active = (time_bins <= CUR_BIN).astype(jnp.float32)
    return (home_force + remote) * active[:, None, :]


def solution(mesh):
    return jax.shard_map(
        local,
        mesh=mesh,
        in_specs=(
            P(("dom", "sub"), None, None),
            P(("dom", "sub"), None),
            P(("dom", "sub")),
            P(("dom", "sub"), None),
            P(("dom", "sub"), None),
            P(None, ("dom", "sub")),
            P(("dom", "sub")),
            P("dom", None),
            P("dom"),
        ),
        out_specs=P(("dom", "sub"), None, None),
        check_vma=False,
    )
```

profile of v0, /device:TPU:1, one launch (start us, length us, event | category | flops | bytes accessed | tf_op | source)
XLA Modules:
  0.0 500.4 jit_solution(13165583080580217074)
XLA Ops:
  3.6 6.4 %all-to-all-start.2 = ((s32[8,1,32]{2,1,0:T(1,128)}), s32[8,1,32]{2,1,0:T(1,128)S(1)}, u32[]{:S(2)}, u32[]{:S(2)}) async-start(s32[8,1,32]{2,1,0:T(1,128)} %broadcast_in_dim.69), calls=%async_computation.2 | async-start | bytes 8192 | tf_op jit(solution)/shard_map/all_to_all | solution.py:15
  10.9 1.5 compare_convert_fusion
  13.4 1.2 all-to-all-done.2
  16.2 20.0 %and_select_fusion.3 = (s32[256]{0:T(256)S(1)}, s32[256]{0:T(256)S(1)}) fusion(s32[256]{0:T(256)S(1)} %get-tuple-element.320, s32[]{:T(128)} %bitcast.53, s32[]{:T(128)} %bitcast.52, s32[256]{0:T(256)S(1)} %reshape.1014, s32[]{:T(128)} %bitcast.51, s32[]{:T(128)} %bitcast.50, s32[]{:T(128)} %bitcast.49, s32[]{:T(128)} %bitcast.48, s32[]{:T(128)} %bitcast.47, ...), kind=kLoop, calls=%fused_computation.221 | loop fusion | flops 19968 | bytes 4224 | tf_op jit(solution)/shard_map/jit(floor_divide)/jit(_where)/select_n | solution.py:184
  37.4 1.9 gather_fusion.8
  39.3 1.9 gather_fusion.9
  42.0 3.9 all-to-all-start.3
  48.3 1.9 gather_fusion.10
  50.4 4.7 all-to-all-start.4
  56.4 3.2 all-to-all-done.4
  62.3 10.6 %all-to-all-start.7 = ((s32[32,1,1]{2,1,0:T(1,128)}), s32[32,1,1]{2,1,0:T(1,128)S(1)}, u32[]{:S(2)}, u32[]{:S(2)}) async-start(s32[32,1,1]{2,1,0:T(1,128)} %bitcast.69), calls=%async_computation.7 | async-start | bytes 32768 | tf_op jit(solution)/shard_map/all_to_all | solution.py:54
  72.9 8.6 %all-to-all-done.7 = s32[32,1,1]{2,1,0:T(1,128)S(1)} async-done(((s32[32,1,1]{2,1,0:T(1,128)}), s32[32,1,1]{2,1,0:T(1,128)S(1)}, u32[]{:S(2)}, u32[]{:S(2)}) %all-to-all-start.7) | async-done | bytes 160 | tf_op jit(solution)/shard_map/all_to_all | solution.py:54
  81.4 3.8 all-to-all-start.9
  85.3 1.9 gather_fusion.11
  87.2 6.6 %all-to-all-done.9 = s32[32,1,1]{2,1,0:T(1,128)S(1)} async-done(((s32[32,1,1]{2,1,0:T(1,128)}), s32[32,1,1]{2,1,0:T(1,128)S(1)}, u32[]{:S(2)}, u32[]{:S(2)}) %all-to-all-start.9) | async-done | bytes 160 | tf_op jit(solution)/shard_map/all_to_all | solution.py:54
  94.6 6.7 %all-to-all-start.1 = ((f32[8,1,4096]{2,1,0:T(1,128)}), f32[8,1,4096]{2,1,0:T(1,128)S(1)}, u32[]{:S(2)}, u32[]{:S(2)}) async-start(f32[8,1,4096]{2,1,0:T(1,128)} %broadcast_in_dim.67), calls=%async_computation.1 | async-start | bytes 262144 | tf_op jit(solution)/shard_map/all_to_all | solution.py:15
  102.3 4.3 all-to-all-done.1
  106.6 4.3 all-to-all-start.5
  113.2 90.5 %gather_fusion.7 = f32[16384]{0:T(1024)S(1)} fusion(f32[32768]{0:T(1024)S(1)} %bitcast.176, s32[16384]{0:T(1024)S(1)} %broadcast_clamp_fusion), kind=kCustom, calls=%fused_computation.7 | custom fusion | bytes 196608 | tf_op jit(solution)/shard_map/gather | solution.py:80
  204.7 5.0 all-to-all-start
  211.9 7.1 %all-to-all-done = f32[8,3,4096]{2,1,0:T(4,128)S(1)} async-done(((f32[8,3,4096]{2,1,0:T(4,128)}), f32[8,3,4096]{2,1,0:T(4,128)S(1)}, u32[]{:S(2)}, u32[]{:S(2)}) %all-to-all-start) | async-done | bytes 393248 | tf_op jit(solution)/shard_map/all_to_all | solution.py:15
  219.0 3.8 all-to-all-start.6
  222.9 8.2 %copy.125 = f32[3,8,4096]{0,2,1:T(8,128)} copy(f32[3,8,4096]{2,0,1:T(4,128)S(1)} %bitcast.188) | data formatting | bytes 786432 | tf_op jit(solution)/shard_map/transpose | solution.py:23
  231.1 60.2 %gather_fusion.6 = f32[16384,3]{1,0:T(8,128)} fusion(f32[3,32768]{0,1:T(8,128)} %bitcast.177, s32[16384]{0:T(1024)S(1)} %broadcast_clamp_fusion), kind=kCustom, calls=%fused_computation.6 | custom fusion | bytes 458752 | tf_op jit(solution)/shard_map/gather | solution.py:79
  291.3 5.3 %copy.126 = f32[64,256,3]{1,2,0:T(4,128)S(1)} copy(f32[64,256,3]{2,1,0:T(8,128)} %bitcast.178) | data formatting | bytes 393216 | tf_op jit(solution)/shard_map/gather | solution.py:79
  297.3 9.2 %all-to-all-start.8 = ((f32[32,1,3,256]{3,1,2,0:T(1,128)}), f32[32,1,3,256]{3,1,2,0:T(1,128)S(1)}, u32[]{:S(2)}, u32[]{:S(2)}) async-start(f32[32,1,3,256]{3,1,2,0:T(1,128)} %copy.144), calls=%async_computation.8 | async-start | bytes 196608 | tf_op jit(solution)/shard_map/all_to_all | solution.py:54
  306.6 37.9 %while.37 = (s32[]{:T(128)}, f32[4,8,3,256]{3,1,0,2:T(8,128)S(1)}, f32[4,8,3,256]{3,1,0,2:T(8,128)S(1)}, s32[4,8]{1,0:T(4,128)S(1)}, f32[64,3,256]{2,1,0:T(4,128...) while((s32[]{:T(128)}, f32[4,8,3,256]{3,1,0,2:T(8,128)S(1)}, ...), condition=%wide.region_18.19_spmd, body=%wide.region_15.18_spmd.sunk | while | flops 45615144 | bytes 8806821 | solution.py:102
  307.2 1.1 fusion.113
  309.0 5.9 %fusion.115 = f32[8,256,256]{2,1,0:T(8,128)S(1)} fusion(f32[8,256,256]{2,1,0:T(8,128)S(1)} %fusion.113, f32[8,256]{1,0:T(8,128)S(1)} %broadcast_multiply_fusion.4), kind=kLoop, calls=%fused_computation.58.clone.1 | loop fusion | flops 36700160 | bytes 4202496 | tf_op jit(solution)/shard_map/while/body/eval_jaxpr/vmap()/div | solution.py:73
  316.7 1.1 fusion.113
  318.5 5.9 %fusion.115 = f32[8,256,256]{2,1,0:T(8,128)S(1)} fusion(f32[8,256,256]{2,1,0:T(8,128)S(1)} %fusion.113, f32[8,256]{1,0:T(8,128)S(1)} %broadcast_multiply_fusion.4), kind=kLoop, calls=%fused_computation.58.clone.1 | loop fusion | flops 36700160 | bytes 4202496 | tf_op jit(solution)/shard_map/while/body/eval_jaxpr/vmap()/div | solution.py:73
  326.2 1.1 fusion.113
  328.0 5.9 %fusion.115 = f32[8,256,256]{2,1,0:T(8,128)S(1)} fusion(f32[8,256,256]{2,1,0:T(8,128)S(1)} %fusion.113, f32[8,256]{1,0:T(8,128)S(1)} %broadcast_multiply_fusion.4), kind=kLoop, calls=%fused_computation.58.clone.1 | loop fusion | flops 36700160 | bytes 4202496 | tf_op jit(solution)/shard_map/while/body/eval_jaxpr/vmap()/div | solution.py:73
  335.7 1.1 fusion.113
  337.5 5.9 %fusion.115 = f32[8,256,256]{2,1,0:T(8,128)S(1)} fusion(f32[8,256,256]{2,1,0:T(8,128)S(1)} %fusion.113, f32[8,256]{1,0:T(8,128)S(1)} %broadcast_multiply_fusion.4), kind=kLoop, calls=%fused_computation.58.clone.1 | loop fusion | flops 36700160 | bytes 4202496 | tf_op jit(solution)/shard_map/while/body/eval_jaxpr/vmap()/div | solution.py:73
  344.5 37.9 %while.38 = (s32[]{:T(128)}, f32[4,8,3,256]{3,1,0,2:T(8,128)S(1)}, f32[4,8,3,256]{3,1,0,2:T(8,128)S(1)}, s32[4,8]{1,0:T(4,128)S(1)}, f32[64,3,256]{2,1,0:T(4,128...) while((s32[]{:T(128)}, f32[4,8,3,256]{3,1,0,2:T(8,128)S(1)}, ...), condition=%wide.region_22.23_spmd, body=%wide.region_19.22_spmd.sunk | while | flops 45615144 | bytes 8806821 | solution.py:102
  345.2 1.1 fusion.117
  347.0 5.9 %fusion.119 = f32[8,256,256]{2,1,0:T(8,128)S(1)} fusion(f32[8,256,256]{2,1,0:T(8,128)S(1)} %fusion.117, f32[8,256]{1,0:T(8,128)S(1)} %broadcast_multiply_fusion.5), kind=kLoop, calls=%fused_computation.93.clone.1 | loop fusion | flops 36700160 | bytes 4202496 | tf_op jit(solution)/shard_map/while/body/eval_jaxpr/vmap()/div | solution.py:73
  354.7 1.1 fusion.117
  356.5 5.9 %fusion.119 = f32[8,256,256]{2,1,0:T(8,128)S(1)} fusion(f32[8,256,256]{2,1,0:T(8,128)S(1)} %fusion.117, f32[8,256]{1,0:T(8,128)S(1)} %broadcast_multiply_fusion.5), kind=kLoop, calls=%fused_computation.93.clone.1 | loop fusion | flops 36700160 | bytes 4202496 | tf_op jit(solution)/shard_map/while/body/eval_jaxpr/vmap()/div | solution.py:73
  364.2 1.1 fusion.117
  366.0 5.9 %fusion.119 = f32[8,256,256]{2,1,0:T(8,128)S(1)} fusion(f32[8,256,256]{2,1,0:T(8,128)S(1)} %fusion.117, f32[8,256]{1,0:T(8,128)S(1)} %broadcast_multiply_fusion.5), kind=kLoop, calls=%fused_computation.93.clone.1 | loop fusion | flops 36700160 | bytes 4202496 | tf_op jit(solution)/shard_map/while/body/eval_jaxpr/vmap()/div | solution.py:73
  373.7 1.1 fusion.117
  375.4 5.9 %fusion.119 = f32[8,256,256]{2,1,0:T(8,128)S(1)} fusion(f32[8,256,256]{2,1,0:T(8,128)S(1)} %fusion.117, f32[8,256]{1,0:T(8,128)S(1)} %broadcast_multiply_fusion.5), kind=kLoop, calls=%fused_computation.93.clone.1 | loop fusion | flops 36700160 | bytes 4202496 | tf_op jit(solution)/shard_map/while/body/eval_jaxpr/vmap()/div | solution.py:73
  383.3 9.2 %all-to-all-start.10 = ((f32[32,2,3,256]{3,1,2,0:T(2,128)}), f32[32,2,3,256]{3,1,2,0:T(2,128)S(1)}, u32[]{:S(2)}, u32[]{:S(2)}) async-start(f32[32,2,3,256]{3,1,2,0:T(2,128)} %copy.149), calls=%async_computation.10 | async-start | bytes 393216 | tf_op jit(solution)/shard_map/all_to_all | solution.py:215
  392.8 9.2 %all-to-all-done.10 = f32[32,2,3,256]{3,1,2,0:T(2,128)S(1)} async-done(((f32[32,2,3,256]{3,1,2,0:T(2,128)}), f32[32,2,3,256]{3,1,2,0:T(2,128)S(1)}, u32[]{:S(2)}, u32[]{:S(2)}) %all-to-all-start.10) | async-done | bytes 196640 | tf_op jit(solution)/shard_map/all_to_all | solution.py:215
  402.0 1.3 gather_fusion.14
  403.3 1.1 copy_multiply_fusion
  404.4 7.0 %all-to-all-start.11 = ((f32[8,32,1,3,256]{4,1,3,2,0:T(8,128)}), f32[8,32,1,3,256]{4,1,3,2,0:T(8,128)S(1)}, u32[]{:S(2)}, u32[]{:S(2)}) async-start(f32[8,32,1,3,256]{4,1,3,2,0:T(8,128)} %copy_multiply_fusion), calls=%async_computation.11 | async-start | bytes 1572864 | tf_op jit(solution)/shard_map/all_to_all | solution.py:220
  411.3 85.0 %while.36 = (s32[]{:T(128)}, f32[8,8,3,256]{3,2,1,0:T(4,128)}, f32[8,8,3,256]{3,2,1,0:T(4,128)S(1)}, s32[8,8]{1,0:T(8,128)}, f32[64,3,256]{2,1,0:T(4,128)S(1)}, /*index=5*/f32[64,256]{1,0:T(8,128)S(1)}, s32[]{:T(128)}) while((s32[]{:T(128)}, f32[8,8,3,256]{3,2,1,0:T(4,128)}, f32[8,8,3,256]{3,2,1,0:T(4,128)S(1)}, s32[8,8]{1,0:T(8,128)}, ...), condition=%wide.region_3.4_spmd, body=%wide.region_0.3_spmd.sunk | while | flops 45613096 | bytes 8692533 | solution.py:102
  412.6 1.1 fusion.110
  414.3 5.9 %fusion.111 = f32[8,256,256]{2,1,0:T(8,128)S(1)} fusion(f32[8,256,256]{2,1,0:T(8,128)S(1)} %fusion.110, f32[8,256]{1,0:T(8,128)S(1)} %gather_fusion.1), kind=kLoop, calls=%fused_computation.28.clone.1 | loop fusion | flops 36700160 | bytes 4202496 | tf_op jit(solution)/shard_map/while/body/eval_jaxpr/vmap()/div | solution.py:73
  423.3 1.1 fusion.110
  425.0 5.9 %fusion.111 = f32[8,256,256]{2,1,0:T(8,128)S(1)} fusion(f32[8,256,256]{2,1,0:T(8,128)S(1)} %fusion.110, f32[8,256]{1,0:T(8,128)S(1)} %gather_fusion.1), kind=kLoop, calls=%fused_computation.28.clone.1 | loop fusion | flops 36700160 | bytes 4202496 | tf_op jit(solution)/shard_map/while/body/eval_jaxpr/vmap()/div | solution.py:73
  433.9 1.1 fusion.110
  435.6 5.9 %fusion.111 = f32[8,256,256]{2,1,0:T(8,128)S(1)} fusion(f32[8,256,256]{2,1,0:T(8,128)S(1)} %fusion.110, f32[8,256]{1,0:T(8,128)S(1)} %gather_fusion.1), kind=kLoop, calls=%fused_computation.28.clone.1 | loop fusion | flops 36700160 | bytes 4202496 | tf_op jit(solution)/shard_map/while/body/eval_jaxpr/vmap()/div | solution.py:73
  444.5 1.1 fusion.110
  446.2 5.9 %fusion.111 = f32[8,256,256]{2,1,0:T(8,128)S(1)} fusion(f32[8,256,256]{2,1,0:T(8,128)S(1)} %fusion.110, f32[8,256]{1,0:T(8,128)S(1)} %gather_fusion.1), kind=kLoop, calls=%fused_computation.28.clone.1 | loop fusion | flops 36700160 | bytes 4202496 | tf_op jit(solution)/shard_map/while/body/eval_jaxpr/vmap()/div | solution.py:73
  455.2 1.1 fusion.110
  456.9 5.9 %fusion.111 = f32[8,256,256]{2,1,0:T(8,128)S(1)} fusion(f32[8,256,256]{2,1,0:T(8,128)S(1)} %fusion.110, f32[8,256]{1,0:T(8,128)S(1)} %gather_fusion.1), kind=kLoop, calls=%fused_computation.28.clone.1 | loop fusion | flops 36700160 | bytes 4202496 | tf_op jit(solution)/shard_map/while/body/eval_jaxpr/vmap()/div | solution.py:73
  467.5 5.9 %fusion.111 = f32[8,256,256]{2,1,0:T(8,128)S(1)} fusion(f32[8,256,256]{2,1,0:T(8,128)S(1)} %fusion.110, f32[8,256]{1,0:T(8,128)S(1)} %gather_fusion.1), kind=kLoop, calls=%fused_computation.28.clone.1 | loop fusion | flops 36700160 | bytes 4202496 | tf_op jit(solution)/shard_map/while/body/eval_jaxpr/vmap()/div | solution.py:73
  478.1 5.9 %fusion.111 = f32[8,256,256]{2,1,0:T(8,128)S(1)} fusion(f32[8,256,256]{2,1,0:T(8,128)S(1)} %fusion.110, f32[8,256]{1,0:T(8,128)S(1)} %gather_fusion.1), kind=kLoop, calls=%fused_computation.28.clone.1 | loop fusion | flops 36700160 | bytes 4202496 | tf_op jit(solution)/shard_map/while/body/eval_jaxpr/vmap()/div | solution.py:73
  488.7 5.9 %fusion.111 = f32[8,256,256]{2,1,0:T(8,128)S(1)} fusion(f32[8,256,256]{2,1,0:T(8,128)S(1)} %fusion.110, f32[8,256]{1,0:T(8,128)S(1)} %gather_fusion.1), kind=kLoop, calls=%fused_computation.28.clone.1 | loop fusion | flops 36700160 | bytes 4202496 | tf_op jit(solution)/shard_map/while/body/eval_jaxpr/vmap()/div | solution.py:73
  496.9 1.3 gather_fusion.15
  (264 shorter events, 78.6 us)
Async XLA Ops:
  3.6 11.0 %all-to-all-start.2 = ((s32[8,1,32]{2,1,0:T(1,128)}), s32[8,1,32]{2,1,0:T(1,128)S(1)}, u32[]{:S(2)}, u32[]{:S(2)}) async-start(s32[8,1,32]{2,1,0:T(1,128)} %broadcast_in_dim.69), calls=%async_computation.2 | async-start | bytes 8192 | tf_op jit(solution)/shard_map/all_to_all | solution.py:15
  14.7 32.1 %copy-start = (f32[64,3,256]{2,0,1:T(8,128)S(1)}, f32[64,3,256]{2,0,1:T(8,128)}, u32[]{:S(2)}) copy-start(f32[64,3,256]{2,0,1:T(8,128)} %param.15) | copy-start | bytes 589828
  36.7 10.2 %copy-start.6 = (s32[64]{0:T(128)S(1)}, s32[64]{0:T(128)}, u32[]{:S(2)}) copy-start(s32[64]{0:T(128)} %param.17) | copy-start | bytes 772
  42.0 8.5 %all-to-all-start.3 = ((s32[8,32,1]{1,2,0:T(1,128)}), s32[8,32,1]{1,2,0:T(1,128)S(1)}, u32[]{:S(2)}, u32[]{:S(2)}) async-start(s32[8,32,1]{1,2,0:T(1,128)} %select_n.234), calls=%async_computation.3 | async-start | bytes 8192 | tf_op jit(solution)/shard_map/all_to_all | solution.py:199
  50.4 9.1 %all-to-all-start.4 = ((s32[8,32,1]{1,2,0:T(1,128)}), s32[8,32,1]{1,2,0:T(1,128)S(1)}, u32[]{:S(2)}, u32[]{:S(2)}) async-start(s32[8,32,1]{1,2,0:T(1,128)} %select_n.236), calls=%async_computation.4 | async-start | bytes 8192 | tf_op jit(solution)/shard_map/all_to_all | solution.py:198
  62.3 19.2 %all-to-all-start.7 = ((s32[32,1,1]{2,1,0:T(1,128)}), s32[32,1,1]{2,1,0:T(1,128)S(1)}, u32[]{:S(2)}, u32[]{:S(2)}) async-start(s32[32,1,1]{2,1,0:T(1,128)} %bitcast.69), calls=%async_computation.7 | async-start | bytes 32768 | tf_op jit(solution)/shard_map/all_to_all | solution.py:54
  81.4 12.4 %all-to-all-start.9 = ((s32[32,1,1]{2,1,0:T(1,128)}), s32[32,1,1]{2,1,0:T(1,128)S(1)}, u32[]{:S(2)}, u32[]{:S(2)}) async-start(s32[32,1,1]{2,1,0:T(1,128)} %bitcast.72), calls=%async_computation.9 | async-start | bytes 32768 | tf_op jit(solution)/shard_map/all_to_all | solution.py:54
  85.3 8.6 %copy-start.4 = (f32[4096]{0:T(1024)S(1)}, f32[4096]{0:T(1024)}, u32[]{:S(2)}) copy-start(f32[4096]{0:T(1024)} %param.21) | copy-start | bytes 49156
  94.6 12.0 %all-to-all-start.1 = ((f32[8,1,4096]{2,1,0:T(1,128)}), f32[8,1,4096]{2,1,0:T(1,128)S(1)}, u32[]{:S(2)}, u32[]{:S(2)}) async-start(f32[8,1,4096]{2,1,0:T(1,128)} %broadcast_in_dim.67), calls=%async_computation.1 | async-start | bytes 262144 | tf_op jit(solution)/shard_map/all_to_all | solution.py:15
  106.6 97.2 %all-to-all-start.5 = ((f32[8,32,1,3,256]{4,1,3,2,0:T(8,128)}), f32[8,32,1,3,256]{4,1,3,2,0:T(8,128)S(1)}, u32[]{:S(2)}, u32[]{:S(2)}) async-start(f32[8,32,1,3,256]{4,1,3,2,0:T(8,128)} %copy_select_fusion), calls=%async_computation.5 | async-start | bytes 1572864 | tf_op jit(solution)/shard_map/all_to_all | solution.py:197
  113.2 90.6 %copy-start.3 = (f32[3,4096]{1,0:T(4,128)S(1)}, f32[3,4096]{1,0:T(4,128)}, u32[]{:S(2)}) copy-start(f32[3,4096]{1,0:T(4,128)} %param.20) | copy-start | bytes 147460
  204.7 18.2 %copy-start.5 = (s32[64]{0:T(128)S(1)}, s32[64]{0:T(128)}, u32[]{:S(2)}) copy-start(s32[64]{0:T(128)} %param.23) | copy-start | bytes 772
  204.7 14.3 %all-to-all-start = ((f32[8,3,4096]{2,1,0:T(4,128)}), f32[8,3,4096]{2,1,0:T(4,128)S(1)}, u32[]{:S(2)}, u32[]{:S(2)}) async-start(f32[8,3,4096]{2,1,0:T(4,128)} %broadcast_in_dim.65), calls=%async_computation | async-start | bytes 1048576 | tf_op jit(solution)/shard_map/all_to_all | solution.py:15
  219.0 78.3 %all-to-all-start.6 = ((f32[32,1,3,256]{3,1,2,0:T(1,128)}), f32[32,1,3,256]{3,1,2,0:T(1,128)S(1)}, u32[]{:S(2)}, u32[]{:S(2)}) async-start(f32[32,1,3,256]{3,1,2,0:T(1,128)} %copy.139), calls=%async_computation.6 | async-start | bytes 196608 | tf_op jit(solution)/shard_map/all_to_all | solution.py:54
  297.3 47.2 %all-to-all-start.8 = ((f32[32,1,3,256]{3,1,2,0:T(1,128)}), f32[32,1,3,256]{3,1,2,0:T(1,128)S(1)}, u32[]{:S(2)}, u32[]{:S(2)}) async-start(f32[32,1,3,256]{3,1,2,0:T(1,128)} %copy.144), calls=%async_computation.8 | async-start | bytes 196608 | tf_op jit(solution)/shard_map/all_to_all | solution.py:54
  383.3 18.6 %all-to-all-start.10 = ((f32[32,2,3,256]{3,1,2,0:T(2,128)}), f32[32,2,3,256]{3,1,2,0:T(2,128)S(1)}, u32[]{:S(2)}, u32[]{:S(2)}) async-start(f32[32,2,3,256]{3,1,2,0:T(2,128)} %copy.149), calls=%async_computation.10 | async-start | bytes 393216 | tf_op jit(solution)/shard_map/all_to_all | solution.py:215
  404.4 92.0 %all-to-all-start.11 = ((f32[8,32,1,3,256]{4,1,3,2,0:T(8,128)}), f32[8,32,1,3,256]{4,1,3,2,0:T(8,128)S(1)}, u32[]{:S(2)}, u32[]{:S(2)}) async-start(f32[8,32,1,3,256]{4,1,3,2,0:T(8,128)} %copy_multiply_fusion), calls=%async_computation.11 | async-start | bytes 1572864 | tf_op jit(solution)/shard_map/all_to_all | solution.py:220
  496.4 1.8 copy-start.2
  496.9 1.7 copy-start.1
where the time goes:
time: 502 us; the launch traced here: 500 us
  local copies, waits for them, and re-layouts  211 us (42%)
  other arithmetic  173 us (34%)
  starting transfers between devices  74.5 us (15%)
  waiting for transfers between devices  40.2 us (8%)
    div x16, other arithmetic, short_pull(): weight = source_mass[:, None] * factor / (range_sq * distance)  94.2 us
    gather x2, local copies, waits for them, and re-layouts, list_tables(): table_mass[lists]  90.6 us
    gather x2, local copies, waits for them, and re-layouts, list_tables(): list_pos = jnp.transpose(table_pos[:, lists], (1, 0, 2))  65.5 us
    all_to_all x4, starting transfers between devices, moved(): lax.all_to_all(group, axis, split_axis=split_dim, concat_axis=concat_dim,...  27.4 us
    select_n x1, other arithmetic, local(): row_slot = row_place // sharers  20 us
    all_to_all x3, starting transfers between devices, sent_to_all(): lax.all_to_all(jnp.broadcast_to(value[None], (length, *value.shape)), axi...  18.1 us
    reduce_sum x16, other arithmetic, short_pull(): range_sq = jnp.sum(offset * offset, axis=0) + soften_sq  17.7 us
    reduce_sum x16, other arithmetic, short_pull(): return -jnp.sum(offset * weight[None, :, :], axis=1)  17.4 us
  transfers between devices with their start and end apart: 12, of which 8 were waited for; matrix products, arithmetic and copies ran while one was open for 61% of the time, Pallas kernels for 0%

commit v1 on v0

--- a/solution.py
+++ b/solution.py
@@ -1,13 +1,12 @@
+import functools
 import jax
 import jax.numpy as jnp
 from jax import lax
+from jax.experimental import pallas as pl
+from jax.experimental.pallas import tpu as pltpu
 from jax.sharding import PartitionSpec as P
 
 CUR_BIN = 2
-
-
-soften_sq = 0.04
-gauss_slope = 1.1283791670955126
 
 
 def sent_to_all(value, axis):
@@ -15,17 +14,6 @@
     return lax.all_to_all(
         jnp.broadcast_to(value[None], (length, *value.shape)), axis, 0, 0, tiled=True
     )
-
-
-def laid_out(blocks, dim):
-    shape = list(blocks.shape[1:])
-    shape[dim] *= blocks.shape[0]
-    return jnp.moveaxis(blocks, 0, dim).reshape(shape)
-
-
-def gathered_copies(value, axis, dim):
-    blocks = sent_to_all(value, axis)
-    return laid_out(blocks, dim)
 
 
 def joined_by_halves(pieces, combine):
@@ -48,67 +36,142 @@
     return joined_by_halves(kept(pieces, identity, value), combine)
 
 
-def grouped_exchange(value, axis, split_dim, concat_dim, work, item_dim, out_dim):
-
-    def moved(group):
-        return lax.all_to_all(group, axis, split_axis=split_dim, concat_axis=concat_dim, tiled=True)
-
-    items = jax.tree.leaves(value)[0].shape[item_dim]
-    ends = [items * k // 2 for k in range(2 + 1)] if items % 2 == 0 else [0, items]
-    groups = [
-        jax.tree.map(lambda a: lax.slice_in_dim(a, low, high, axis=item_dim), value)
-        for low, high in zip(ends, ends[1:])
-    ]
-    arrived = [moved(group) for group in groups]
-    made = [work(group) for group in arrived]
-    return jax.tree.map(lambda *parts: jnp.concatenate(parts, axis=out_dim), *made)
-
-
-def short_pull(sink_pos, source_pos, source_mass):
-    offset = sink_pos[:, None, :] - source_pos[:, :, None]
-    range_sq = jnp.sum(offset * offset, axis=0) + soften_sq
-    distance = jnp.sqrt(range_sq)
-    scaled = distance * 0.5
-    factor = lax.erfc(scaled) + gauss_slope * scaled * jnp.exp(-scaled * scaled)
-    weight = source_mass[:, None] * factor / (range_sq * distance)
-    return -jnp.sum(offset * weight[None, :, :], axis=1)
-
-
-def list_tables(table_pos, table_mass, lists, counts):
-    entry_ids = jnp.arange(lists.shape[1], dtype=jnp.int32)
-    list_pos = jnp.transpose(table_pos[:, lists], (1, 0, 2))
-    list_mass = table_mass[lists] * (entry_ids[None, :] < counts[:, None]).astype(jnp.float32)
-    return (list_pos, list_mass)
-
-
-def evaluate(sink_pos, list_rows, is_alive, list_pos, list_mass):
-    item_count = sink_pos.shape[0]
-    padded = -(-item_count // 8) * 8
-    padding = padded - item_count
-    if padding:
-        sink_pos = jnp.concatenate(
-            [sink_pos, jnp.zeros((padding,) + sink_pos.shape[1:], sink_pos.dtype)]
+CHUNK = 32
+LOG2E = 1.4426950408889634
+SLOPE = 1.1283791670955126
+GROUPS = 64
+LIST = 256
+MIN_STEPS = 2
+
+
+def pair_sums(xs, node, acc):
+    out = list(acc)
+    for g in range(CHUNK // 8):
+        rows = slice(8 * g, 8 * g + 8)
+        d = [xs[c] - jnp.concatenate([node[c][rows]] * 2, axis=1) for c in range(3)]
+        s = d[0] * d[0] + (d[1] * d[1] + (d[2] * d[2] + 0.01))
+        inv = lax.rsqrt(s)
+        e = jnp.exp2(s * (-LOG2E))
+        tail = 1.0 - lax.erf(s * inv)
+        m = jnp.concatenate([node[3][rows]] * 2, axis=1)
+        w = (inv * tail + SLOPE * e) * (inv * inv) * m
+        out = [out[c] + d[c] * w for c in range(3)]
+    return tuple(out)
+
+
+def compute_kernel(rows_ref, counts_ref, pos_ref, table_ref, out_ref, cols, first):
+    V = rows_ref.shape[0]
+
+    def turn(l, carry):
+        t = table_ref[l]
+        t = jnp.concatenate([t, t], axis=0)
+        cols[l, :, 0:8] = t.T
+        return carry
+    lax.fori_loop(0, GROUPS, turn, 0, unroll=8)
+
+    def fetch(row, i):
+        n = cols[row, CHUNK * i:CHUNK * (i + 1), 0:8]
+        return tuple(jnp.broadcast_to(n[:, c:c + 1], (CHUNK, 128)) for c in range(4))
+
+    def prefetch(v):
+        row = jnp.maximum(rows_ref[v], 0)
+        for c, col in enumerate(fetch(row, 0)):
+            first[c] = col
+    prefetch(0)
+
+    def visit(v, carry):
+        row = rows_ref[v]
+        nxt = jnp.minimum(v + 1, V - 1)
+        safe = jnp.maximum(row, 0)
+        steps = (counts_ref[safe] + (CHUNK - 1)) // CHUNK
+        index = jnp.where(row < 0, 0, jnp.clip(steps - (MIN_STEPS - 1), 1, LIST // CHUNK - MIN_STEPS + 1))
+
+        def dead():
+            prefetch(nxt)
+            out_ref[v] = jnp.zeros((3, 256), jnp.float32)
+
+        def alive(n):
+            def run():
+                x = pos_ref[v] * 0.5
+                xs = [jnp.broadcast_to(x[c:c + 1], (8, 256)) for c in range(3)]
+                zero = jnp.zeros((8, 256), jnp.float32)
+                acc = (zero, zero, zero)
+                acc = pair_sums(xs, tuple(first[c] for c in range(4)), acc)
+                prefetch(nxt)
+                for i in range(1, n):
+                    acc = pair_sums(xs, fetch(safe, i), acc)
+                out_ref[v] = jnp.concatenate([jnp.sum(a, axis=0, keepdims=True) for a in acc], axis=0)
+            return run
+        lax.switch(index, [dead] + [alive(n) for n in range(MIN_STEPS, LIST // CHUNK + 1)])
+        return carry
+    lax.fori_loop(0, V, visit, 0)
+
+
+def compute(rows, counts, pos, table):
+    V = rows.shape[0]
+    return pl.pallas_call(
+        compute_kernel,
+        out_shape=jax.ShapeDtypeStruct((V, 3, 256), jnp.float32),
+        in_specs=[pl.BlockSpec(memory_space=pltpu.SMEM)] * 2 + [pl.BlockSpec(memory_space=pltpu.VMEM)] * 2,
+        out_specs=pl.BlockSpec(memory_space=pltpu.VMEM),
+        scratch_shapes=[pltpu.VMEM((GROUPS, LIST, 128), jnp.float32), pltpu.VMEM((4, CHUNK, 128), jnp.float32)],
+        compiler_params=pltpu.CompilerParams(vmem_limit_bytes=48 * 2**20),
+    )(rows, counts, pos, table)
+
+
+def gather_kernel(lists_ref, counts_ref, nodes_ref, table_ref, tiles, pieces):
+    owners = nodes_ref.shape[0]
+    per_owner = nodes_ref.shape[2] // 128
+    for o in range(owners):
+        for j in range(per_owner):
+            tiles[o * per_owner + j] = nodes_ref[o, :, 128 * j:128 * (j + 1)]
+    for c in range(4):
+        left = tiles[:, c, :].T
+        for p in range(3):
+            part = left.astype(jnp.bfloat16)
+            pieces[p, 128 * c:128 * (c + 1), :] = part
+            left = left - part.astype(jnp.float32)
+    highs = owners * per_owner
+
+    def one_list(l, carry):
+        index = lists_ref[pl.ds(l, 1), :]
+        high = lax.shift_right_logical(index, 7)
+        low = jnp.bitwise_and(index, 127)
+        pick = (lax.broadcasted_iota(jnp.int32, (highs, LIST), 0) == high)
+        pick = jnp.where(pick, 1.0, 0.0).astype(jnp.bfloat16)
+        rows = jnp.zeros((512, LIST), jnp.float32)
+        for p in range(3):
+            rows = rows + jnp.dot(pieces[p], pick, preferred_element_type=jnp.float32)
+        here = lax.broadcasted_iota(jnp.int32, (128, LIST), 0) == low
+        valid = lax.broadcasted_iota(jnp.int32, (1, LIST), 1) < counts_ref[l]
+        picked = [
+            jnp.sum(jnp.where(here, rows[128 * c:128 * (c + 1)], 0.0), axis=0, keepdims=True)
+            for c in range(4)
+        ]
+        table_ref[l] = jnp.concatenate(
+            [0.5 * picked[0], 0.5 * picked[1], 0.5 * picked[2], jnp.where(valid, -0.25 * picked[3], 0.0)], axis=0
         )
-        list_rows = jnp.concatenate([list_rows, jnp.zeros((padding,), jnp.int32)])
-        is_alive = jnp.concatenate([is_alive, jnp.zeros((padding,), jnp.float32)])
-
-    def one_item(sink_one, list_row, alive_one):
-        return short_pull(sink_one, list_pos[list_row], list_mass[list_row] * alive_one)
-
-    def one_group(operands):
-        return jax.vmap(one_item)(*operands)
-
-    width = sink_pos.shape[2]
-    grouped = lax.map(
-        one_group,
-        (
-            sink_pos.reshape(padded // 8, 8, 3, width),
-            list_rows.reshape(padded // 8, 8),
-            is_alive.reshape(padded // 8, 8),
-        ),
-    )
-    return grouped.reshape(padded, 3, width)[:item_count]
-
+        return carry
+    lax.fori_loop(0, lists_ref.shape[0], one_list, 0)
+
+
+def gather_lists(lists, counts, nodes):
+    owners, _, per = nodes.shape
+    return pl.pallas_call(
+        gather_kernel,
+        out_shape=jax.ShapeDtypeStruct((lists.shape[0], 4, LIST), jnp.float32),
+        in_specs=[
+            pl.BlockSpec(memory_space=pltpu.VMEM),
+            pl.BlockSpec(memory_space=pltpu.SMEM),
+            pl.BlockSpec(memory_space=pltpu.VMEM),
+        ],
+        out_specs=pl.BlockSpec(memory_space=pltpu.VMEM),
+        scratch_shapes=[
+            pltpu.VMEM((owners * per // 128, 4, 128), jnp.float32),
+            pltpu.VMEM((3, 512, owners * per // 128), jnp.bfloat16),
+        ],
+        compiler_params=pltpu.CompilerParams(vmem_limit_bytes=48 * 2**20),
+    )(lists, counts, nodes)
 
 def ranks_within(bucket, usable, bucket_count):
     onehot = (
@@ -146,26 +209,22 @@
     blocks, most_visits = targets.shape
     width = positions.shape[2]
     capacity = max(2, blocks * most_visits // domains)
-    table_pos, table_mass = (
-        gathered_copies(node_pos, "sub", 1),
-        gathered_copies(node_mass, "sub", 0),
-    )
-    list_pos, list_mass = list_tables(table_pos, table_mass, node_lists, list_counts)
-    home_force = evaluate(
-        positions, home_groups, jnp.ones((blocks,), jnp.float32), list_pos, list_mass
-    )
+    nodes = lax.all_gather(jnp.concatenate([node_pos, node_mass[None]], axis=0), "sub")
+    share = GROUPS // sharers
+    mine = lax.axis_index("sub") * share
+    piece = gather_lists(
+        lax.dynamic_slice_in_dim(node_lists, mine, share),
+        lax.dynamic_slice_in_dim(list_counts, mine, share),
+        nodes,
+    )
+    table = lax.all_gather(piece, "sub", tiled=True)
+    home_force = compute(home_groups, list_counts, positions, table)
 
     def imported(arrived):
         arrived_pos, arrived_group = arrived
         leading = arrived_group.shape
         flat_group = arrived_group.reshape(-1)
-        pulled = evaluate(
-            arrived_pos.reshape((-1, 3, width)),
-            jnp.maximum(flat_group, 0),
-            (flat_group >= 0).astype(jnp.float32),
-            list_pos,
-            list_mass,
-        )
+        pulled = compute(flat_group, list_counts, arrived_pos.reshape((-1, 3, width)), table)
         return pulled.reshape(leading + (3, width))
 
     flat_dest = targets.reshape(-1)
@@ -211,7 +270,9 @@
     mid_group = jnp.where(second_filled, arrival_group[arrival_row], -1).reshape(
         domains, second_width
     )
-    computed = grouped_exchange((mid_pos, mid_group), "dom", 0, 0, imported, 1, 1)
+    computed = imported(
+        tuple(lax.all_to_all(a, "dom", split_axis=0, concat_axis=0, tiled=True) for a in (mid_pos, mid_group))
+    )
     returned = lax.all_to_all(computed, "dom", split_axis=0, concat_axis=0, tiled=True)
     arrival_force = returned.reshape(domains * second_width, 3, width)[
         jnp.where(arrival_ok, second_index, 0)

time: 502 us -> 211 us (0.42)
  local copies, waits for them, and re-layouts: 211 us -> 24.6 us
  other arithmetic: 173 us -> 27.2 us
  Pallas kernels: 0 us -> 48.4 us
  blocking collectives: 0 us -> 28.2 us
  starting transfers between devices: 74.5 us -> 46.6 us
  waiting for transfers between devices: 40.2 us -> 33.4 us
    gather x36 -> x0, local copies, waits for them, and re-layouts: 175 us -> none  [the longest x2 90.6 us: list_tables(): table_mass[lists]]
    div x16 -> x0, other arithmetic: 94.2 us -> none  [short_pull(): weight = source_mass[:, None] * factor / (range_sq * distance)]
    pallas_call x0 -> x3, Pallas kernels: none -> 48.4 us  [the longest x2 44.3 us: compute(): pl.pallas_call(compute_kernel, out_shape=jax.ShapeDtypeStruct((V, 3, 256)...]
    reduce_sum x32 -> x0, other arithmetic: 35.1 us -> none  [the longest x16 17.7 us: short_pull(): range_sq = jnp.sum(offset * offset, axis=0) + soften_sq]
    all_gather x0 -> x2, blocking collectives: none -> 28.2 us  [the longest x1 15.3 us: local(): lax.all_gather(jnp.concatenate([node_pos, node_mass[None]], axis=0), 'sub')]
    all_to_all x4 -> x2, starting transfers between devices: 27.4 us -> 14.4 us  [local(): lax.all_to_all(a, 'dom', split_axis=0, concat_axis=0, tiled=True)]
    all_to_all x3 -> x1, starting transfers between devices: 18.1 us -> 6.41 us  [sent_to_all(): lax.all_to_all(jnp.broadcast_to(value[None], (length, *value.shape)), axi...]
    all_to_all x1, waiting for transfers between devices: 0.01 us -> 9.64 us  [local(): lax.all_to_all(out_pos, 'sub', split_axis=0, concat_axis=0, tiled=True)]
  transfers between devices with their start and end apart: 12 -> 8, of which waited for: 8 -> 6; matrix products, arithmetic and copies ran while one was open for 61% -> 5% of each run, Pallas kernels for 0% -> 12%
where the time goes in v1:
time: 211 us; the launch traced here: 209 us
  Pallas kernels  48.4 us (23%)
  starting transfers between devices  46.6 us (22%)
  waiting for transfers between devices  33.4 us (16%)
  blocking collectives  28.2 us (13%)
  other arithmetic  27.2 us (13%)
  local copies, waits for them, and re-layouts  24.6 us (12%)
    pallas_call x2, Pallas kernels, compute(): pl.pallas_call(compute_kernel, out_shape=jax.ShapeDtypeStruct((V, 3, 256)...  44.3 us
    select_n x1, other arithmetic, local(): row_slot = row_place // sharers  20.1 us
    all_gather x1, blocking collectives, local(): lax.all_gather(jnp.concatenate([node_pos, node_mass[None]], axis=0), 'sub')  15.3 us
    all_to_all x2, starting transfers between devices, local(): lax.all_to_all(a, 'dom', split_axis=0, concat_axis=0, tiled=True)  14.4 us
    all_gather x1, blocking collectives, local(): table = lax.all_gather(piece, 'sub', tiled=True)  12.8 us
    all_to_all x1, waiting for transfers between devices, local(): lax.all_to_all(out_pos, 'sub', split_axis=0, concat_axis=0, tiled=True)  9.64 us
    all_to_all x1, waiting for transfers between devices, local(): lax.all_to_all(computed, 'dom', split_axis=0, concat_axis=0, tiled=True)  9.17 us
    all_to_all x1, starting transfers between devices, local(): lax.all_to_all(computed, 'dom', split_axis=0, concat_axis=0, tiled=True)  7.49 us
  transfers between devices with their start and end apart: 8, of which 6 were waited for; matrix products, arithmetic and copies ran while one was open for 5% of the time, Pallas kernels for 12%

profile of v1, /device:TPU:1, one launch (start us, length us, event | category | flops | bytes accessed | tf_op | source)
XLA Modules:
  0.0 208.8 jit_solution(2753427370918576249)
XLA Ops:
  0.0 0.8 fusion.33
  1.0 0.1 ge.56
  1.5 0.6 reduce-window.14
  2.0 0.2 slice_reduce_fusion
  2.3 0.2 convert_reduce_fusion
  2.4 0.6 broadcast_in_dim.54
  3.0 6.4 %all-to-all-start = ((s32[8,1,32]{2,1,0:T(1,128)}), s32[8,1,32]{2,1,0:T(1,128)S(1)}, u32[]{:S(2)}, u32[]{:S(2)}) async-start(s32[8,1,32]{2,1,0:T(1,128)} %broadcast_in_dim.54), calls=%async_computation | async-start | bytes 8192 | tf_op jit(solution)/shard_map/all_to_all | solution.py:14
  9.5 0.1 copy.106
  9.7 0.5 copy-done.8
  10.4 3.6 %all-to-all-done = s32[8,1,32]{2,1,0:T(1,128)S(1)} async-done(((s32[8,1,32]{2,1,0:T(1,128)}), s32[8,1,32]{2,1,0:T(1,128)S(1)}, u32[]{:S(2)}, u32[]{:S(2)}) %all-to-all-start) | async-done | bytes 1056 | tf_op jit(solution)/shard_map/all_to_all | solution.py:14
  14.2 0.7 fusion.34
  14.9 0.7 fusion.35
  15.6 20.1 %and_select_fusion.3 = (s32[256]{0:T(256)S(1)}, s32[256]{0:T(256)S(1)}) fusion(s32[256]{0:T(256)S(1)} %get-tuple-element.6, s32[]{:T(128)} %bitcast.34, s32[]{:T(128)} %bitcast.33, s32[256]{0:T(256)S(1)} %reshape.488, s32[]{:T(128)} %bitcast.32, s32[]{:T(128)} %bitcast.31, s32[]{:T(128)} %bitcast.30, s32[]{:T(128)} %bitcast.29, s32[]{:T(128)} %bitcast.28, ...), kind=kLoop, calls=%fused_computation.98 | loop fusion | flops 19968 | bytes 4224 | tf_op jit(solution)/shard_map/jit(floor_divide)/jit(_where)/select_n | solution.py:243
  35.8 0.3 fusion
  36.3 0.2 fusion.2
  36.5 0.1 select_reduce_fusion
  36.7 0.1 fusion.6
  36.8 1.9 gather_fusion.3
  38.9 1.9 gather_fusion
  40.8 1.9 gather_fusion.1
  42.8 0.7 select_n.202
  43.5 3.9 %all-to-all-start.1 = ((s32[8,32,1]{1,2,0:T(1,128)}), s32[8,32,1]{1,2,0:T(1,128)S(1)}, u32[]{:S(2)}, u32[]{:S(2)}) async-start(s32[8,32,1]{1,2,0:T(1,128)} %select_n.202), calls=%async_computation.1 | async-start | bytes 8192 | tf_op jit(solution)/shard_map/all_to_all | solution.py:258
  47.4 1.9 gather_fusion.4
  49.3 1.0 copy_select_fusion
  50.3 0.7 select_n.204
  51.0 0.9 all-to-all-done.1
  51.9 3.9 %all-to-all-start.2 = ((s32[8,32,1]{1,2,0:T(1,128)}), s32[8,32,1]{1,2,0:T(1,128)S(1)}, u32[]{:S(2)}, u32[]{:S(2)}) async-start(s32[8,32,1]{1,2,0:T(1,128)} %select_n.204), calls=%async_computation.2 | async-start | bytes 8192 | tf_op jit(solution)/shard_map/all_to_all | solution.py:257
  55.9 0.5 broadcast.665
  56.3 0.6 reduce.15
  57.0 3.5 %all-to-all-done.2 = s32[8,32,1]{1,2,0:T(1,128)S(1)} async-done(((s32[8,32,1]{1,2,0:T(1,128)}), s32[8,32,1]{1,2,0:T(1,128)S(1)}, u32[]{:S(2)}, u32[]{:S(2)}) %all-to-all-start.2) | async-done | bytes 1056 | tf_op jit(solution)/shard_map/all_to_all | solution.py:257
  60.5 4.1 %all-to-all-start.4 = ((f32[8,32,1,3,256]{4,1,3,2,0:T(8,128)}), f32[8,32,1,3,256]{4,1,3,2,0:T(8,128)S(1)}, u32[]{:S(2)}, u32[]{:S(2)}) async-start(f32[8,32,1,3,256]{4,1,3,2,0:T(8,128)} %copy_select_fusion), calls=%async_computation.4 | async-start | bytes 1572864 | tf_op jit(solution)/shard_map/all_to_all | solution.py:256
  64.6 0.6 reduce.16
  65.4 0.1 broadcast_in_dim.58
  65.5 0.1 select_reduce_fusion.1
  65.7 0.8 gather_fusion.2
  66.5 0.7 select_n.207
  67.2 9.6 %all-to-all-done.4 = f32[8,32,1,3,256]{4,1,3,2,0:T(8,128)S(1)} async-done(((f32[8,32,1,3,256]{4,1,3,2,0:T(8,128)}), f32[8,32,1,3,256]{4,1,3,2,0:T(8,128)S(1)}, u32[]{:S(2)}, u32[]{:S(2)}) %all-to-all-start.4) | async-done | bytes 786464 | tf_op jit(solution)/shard_map/all_to_all | solution.py:256
  76.8 10.6 %all-to-all-start.3 = ((s32[32,1,2]{2,1,0:T(1,128)}), s32[32,1,2]{2,1,0:T(1,128)S(1)}, u32[]{:S(2)}, u32[]{:S(2)}) async-start(s32[32,1,2]{2,1,0:T(1,128)} %bitcast.44), calls=%async_computation.3 | async-start | bytes 32768 | tf_op jit(solution)/shard_map/all_to_all | solution.py:274
  87.4 0.5 copy.111
  87.9 0.7 gather_fusion.5
  88.6 0.8 copy_select_fusion.1
  89.5 6.5 %all-to-all-done.3 = s32[32,1,2]{2,1,0:T(1,128)S(1)} async-done(((s32[32,1,2]{2,1,0:T(1,128)}), s32[32,1,2]{2,1,0:T(1,128)S(1)}, u32[]{:S(2)}, u32[]{:S(2)}) %all-to-all-start.3) | async-done | bytes 288 | tf_op jit(solution)/shard_map/all_to_all | solution.py:274
  96.0 3.9 %all-to-all-start.5 = ((f32[32,2,3,256]{3,1,2,0:T(2,128)}), f32[32,2,3,256]{3,1,2,0:T(2,128)S(1)}, u32[]{:S(2)}, u32[]{:S(2)}) async-start(f32[32,2,3,256]{3,1,2,0:T(2,128)} %copy_select_fusion.1), calls=%async_computation.5 | async-start | bytes 393216 | tf_op jit(solution)/shard_map/all_to_all | solution.py:274
  100.0 0.6 copy-done.1
  100.7 15.3 %all-gather.1.nodes_ref = f32[8,4,4096]{2,1,0:T(4,128)S(1)} all-gather(f32[1,4,4096]{2,1,0:T(4,128)S(1)} %maximum_bitcast_fusion), channel_id=2, replica_groups=mesh['dom'=32,'sub'=8] {'sub'}, dimensions={0}, use_global_device_ids=true | all-gather | bytes 589824 | tf_op jit(solution)/shard_map/all_gather | solution.py:212
  116.0 4.1 %shard_map.91 = f32[8,4,256]{2,1,0:T(4,128)S(1)} custom-call(s32[8,256]{1,0:T(8,128)S(1)} %constant_dynamic-slice_fusion.lists_ref, s32[8]{0:T(128)S(1)} %dynamic_slice.7.counts_ref, f32[8,4,4096]{2,1,0:T(4,128)S(1)} %all-gather.1.nodes_ref), custom_call_target="tpu_custom_call" | custom-call | tf_op jit(solution)/shard_map/pallas_call | solution.py:160
  120.0 12.8 %all_gather.11.table_ref = f32[64,4,256]{2,1,0:T(4,128)S(1)} all-gather(f32[8,4,256]{2,1,0:T(4,128)S(1)} %shard_map.91), channel_id=1, replica_groups=mesh['dom'=32,'sub'=8] {'sub'}, dimensions={0}, use_global_device_ids=true | all-gather | bytes 294912 | tf_op jit(solution)/shard_map/all_gather | solution.py:220
  132.9 0.6 reduce.17
  133.7 22.4 %shard_map.93 = f32[64,3,256]{2,1,0:T(4,128)S(1)} custom-call(s32[64]{0:T(128)S(1)} %reshape.477.rows_ref, s32[64]{0:T(128)S(1)} %copy-done.1, f32[64,3,256]{2,1,0:T(4,128)S(1)} %bitcast.89, f32[64,4,256]{2,1,0:T(4,128)S(1)} %all_gather.11.table_ref), custom_call_target="tpu_custom_call" | custom-call | tf_op jit(solution)/shard_map/pallas_call | solution.py:112
  156.1 0.8 copy.114
  156.9 7.5 %all-to-all-start.6 = ((f32[32,2,3,256]{3,1,2,0:T(2,128)}), f32[32,2,3,256]{3,1,2,0:T(2,128)S(1)}, u32[]{:S(2)}, u32[]{:S(2)}) async-start(f32[32,2,3,256]{3,1,2,0:T(2,128)} %copy.114), calls=%async_computation.6 | async-start | bytes 393216 | tf_op jit(solution)/shard_map/all_to_all | solution.py:276
  164.6 9.2 %all-to-all-done.6 = f32[32,2,3,256]{3,1,2,0:T(2,128)S(1)} async-done(((f32[32,2,3,256]{3,1,2,0:T(2,128)}), f32[32,2,3,256]{3,1,2,0:T(2,128)S(1)}, u32[]{:S(2)}, u32[]{:S(2)}) %all-to-all-start.6) | async-done | bytes 196640 | tf_op jit(solution)/shard_map/all_to_all | solution.py:276
  173.9 1.3 gather_fusion.6
  175.1 0.2 copy.117
  175.3 0.1 broadcast_multiply_fusion
  175.4 1.0 copy.118
  176.4 6.3 %all-to-all-start.7 = ((f32[8,32,1,3,256]{4,1,3,2,0:T(8,128)}), f32[8,32,1,3,256]{4,1,3,2,0:T(8,128)S(1)}, u32[]{:S(2)}, u32[]{:S(2)}) async-start(f32[8,32,1,3,256]{4,1,3,2,0:T(8,128)} %copy.118), calls=%async_computation.7 | async-start | bytes 1572864 | tf_op jit(solution)/shard_map/all_to_all | solution.py:281
  182.9 0.1 copy.99.pos_ref
  183.2 0.5 copy-done.2
  183.7 21.9 %shard_map.92 = f32[64,3,256]{2,1,0:T(4,128)S(1)} custom-call(s32[64]{0:T(128)S(1)} %copy-done.2, s32[64]{0:T(128)S(1)} %copy-done.1, f32[64,3,256]{2,1,0:T(4,128)S(1)} %copy.99.pos_ref, f32[64,4,256]{2,1,0:T(4,128)S(1)} %all_gather.11.table_ref), custom_call_target="tpu_custom_call" | custom-call | tf_op jit(solution)/shard_map/pallas_call | solution.py:112
  205.8 0.5 copy.122
  206.3 1.3 gather_fusion.7
  207.6 0.4 multiply_reduce_fusion
  208.1 0.7 copy.124
  (81 shorter events, 2.8 us)
Async XLA Ops:
  0.0 99.9 %copy-start = (s32[64,256]{1,0:T(8,128)S(1)}, s32[64,256]{1,0:T(8,128)}, u32[]{:S(2)}) copy-start(s32[64,256]{1,0:T(8,128)} %param.16) | copy-start | bytes 196612
  0.0 0.8 copy-start.7
  2.0 7.4 %copy-start.4 = (f32[3,4096]{1,0:T(4,128)S(1)}, f32[3,4096]{1,0:T(4,128)}, u32[]{:S(2)}) copy-start(f32[3,4096]{1,0:T(4,128)} %param.14) | copy-start | bytes 147460
  2.4 7.0 %copy-start.6 = (f32[4096]{0:T(1024)S(1)}, f32[4096]{0:T(1024)}, u32[]{:S(2)}) copy-start(f32[4096]{0:T(1024)} %param.15) | copy-start | bytes 49156
  3.0 11.0 %all-to-all-start = ((s32[8,1,32]{2,1,0:T(1,128)}), s32[8,1,32]{2,1,0:T(1,128)S(1)}, u32[]{:S(2)}, u32[]{:S(2)}) async-start(s32[8,1,32]{2,1,0:T(1,128)} %broadcast_in_dim.54), calls=%async_computation | async-start | bytes 8192 | tf_op jit(solution)/shard_map/all_to_all | solution.py:14
  9.5 0.7 copy-start.8
  40.8 6.6 %copy-start.3 = (f32[64,3,256]{2,0,1:T(8,128)S(1)}, f32[64,3,256]{2,0,1:T(8,128)}, u32[]{:S(2)}) copy-start(f32[64,3,256]{2,0,1:T(8,128)} %param.9) | copy-start | bytes 589828
  43.5 8.5 %all-to-all-start.1 = ((s32[8,32,1]{1,2,0:T(1,128)}), s32[8,32,1]{1,2,0:T(1,128)S(1)}, u32[]{:S(2)}, u32[]{:S(2)}) async-start(s32[8,32,1]{1,2,0:T(1,128)} %select_n.202), calls=%async_computation.1 | async-start | bytes 8192 | tf_op jit(solution)/shard_map/all_to_all | solution.py:258
  51.9 8.5 %all-to-all-start.2 = ((s32[8,32,1]{1,2,0:T(1,128)}), s32[8,32,1]{1,2,0:T(1,128)S(1)}, u32[]{:S(2)}, u32[]{:S(2)}) async-start(s32[8,32,1]{1,2,0:T(1,128)} %select_n.204), calls=%async_computation.2 | async-start | bytes 8192 | tf_op jit(solution)/shard_map/all_to_all | solution.py:257
  60.5 16.3 %all-to-all-start.4 = ((f32[8,32,1,3,256]{4,1,3,2,0:T(8,128)}), f32[8,32,1,3,256]{4,1,3,2,0:T(8,128)S(1)}, u32[]{:S(2)}, u32[]{:S(2)}) async-start(f32[8,32,1,3,256]{4,1,3,2,0:T(8,128)} %copy_select_fusion), calls=%async_computation.4 | async-start | bytes 1572864 | tf_op jit(solution)/shard_map/all_to_all | solution.py:256
  76.8 19.2 %all-to-all-start.3 = ((s32[32,1,2]{2,1,0:T(1,128)}), s32[32,1,2]{2,1,0:T(1,128)S(1)}, u32[]{:S(2)}, u32[]{:S(2)}) async-start(s32[32,1,2]{2,1,0:T(1,128)} %bitcast.44), calls=%async_computation.3 | async-start | bytes 32768 | tf_op jit(solution)/shard_map/all_to_all | solution.py:274
  96.0 37.6 %all-to-all-start.5 = ((f32[32,2,3,256]{3,1,2,0:T(2,128)}), f32[32,2,3,256]{3,1,2,0:T(2,128)S(1)}, u32[]{:S(2)}, u32[]{:S(2)}) async-start(f32[32,2,3,256]{3,1,2,0:T(2,128)} %copy_select_fusion.1), calls=%async_computation.5 | async-start | bytes 393216 | tf_op jit(solution)/shard_map/all_to_all | solution.py:274
  99.9 0.7 copy-start.1
  156.9 16.9 %all-to-all-start.6 = ((f32[32,2,3,256]{3,1,2,0:T(2,128)}), f32[32,2,3,256]{3,1,2,0:T(2,128)S(1)}, u32[]{:S(2)}, u32[]{:S(2)}) async-start(f32[32,2,3,256]{3,1,2,0:T(2,128)} %copy.114), calls=%async_computation.6 | async-start | bytes 393216 | tf_op jit(solution)/shard_map/all_to_all | solution.py:276
  176.4 29.3 %all-to-all-start.7 = ((f32[8,32,1,3,256]{4,1,3,2,0:T(8,128)}), f32[8,32,1,3,256]{4,1,3,2,0:T(8,128)S(1)}, u32[]{:S(2)}, u32[]{:S(2)}) async-start(f32[8,32,1,3,256]{4,1,3,2,0:T(8,128)} %copy.118), calls=%async_computation.7 | async-start | bytes 1572864 | tf_op jit(solution)/shard_map/all_to_all | solution.py:281
  183.1 0.7 copy-start.2
  183.7 21.9 %copy-start.5 = (s32[64,256]{1,0:T(8,128)S(1)}, s32[64,256]{1,0:T(8,128)}, u32[]{:S(2)}) copy-start(s32[64,256]{1,0:T(8,128)} %param.10) | copy-start | bytes 196612

commit v2 on v1

v2 whole, which is shorter than its diff:
```python
import jax
import jax.numpy as jnp
from jax import lax
from jax.experimental import pallas as pl
from jax.experimental.pallas import tpu as pltpu
from jax.sharding import PartitionSpec as P

CUR_BIN = 2
CHUNK = 32
LOG2E = 1.4426950408889634
SLOPE = 1.1283791670955126
GROUPS = 64
LIST = 256
MIN_STEPS = 2
N_DOM = 32
N_SUB = 8
TOP = 4
BLK = 64
NODE_DEV = 4096
SHARE = GROUPS // N_SUB
MESH = pl.DeviceIdType.MESH
F32 = jnp.float32
BF16 = jnp.bfloat16


def thirds(value):
    parts = []
    for _ in range(3):
        part = value.astype(BF16)
        parts.append(part)
        value = value - part.astype(F32)
    return parts


def greet(me_dom, me_sub):
    barrier = pltpu.get_barrier_semaphore()
    for p in range(1, N_SUB):
        pl.semaphore_signal(
            barrier, inc=1, device_id={"sub": lax.rem(me_sub + p, N_SUB)}, device_id_type=MESH
        )

    def one(i, carry):
        pl.semaphore_signal(
            barrier, inc=1, device_id={"dom": lax.rem(me_dom + i, N_DOM)}, device_id_type=MESH
        )
        return carry

    lax.fori_loop(1, N_DOM, one, 0)
    return barrier


def to_sub(src, dst, send, recv, peer, slot, mine):
    return pltpu.make_async_remote_copy(
        src_ref=src,
        dst_ref=dst.at[slot],
        send_sem=send.at[peer],
        recv_sem=recv.at[slot],
        device_id={"sub": peer},
        device_id_type=MESH,
    )


def start_sub(src_of, dst, send, recv, me):
    for p in range(1, N_SUB):
        peer = lax.rem(me + p, N_SUB)
        to_sub(src_of(peer), dst, send, recv, peer, me, me).start()


def wait_sub_recv(src_of, dst, send, recv, me):
    for p in range(1, N_SUB):
        peer = lax.rem(me + p, N_SUB)
        to_sub(src_of(peer), dst, send, recv, peer, peer, me).wait_recv()


def wait_sub_send(src_of, dst, send, recv, me):
    for p in range(1, N_SUB):
        peer = lax.rem(me + p, N_SUB)
        to_sub(src_of(peer), dst, send, recv, peer, me, me).wait_send()


def dom_copy(src, dst, send, recv, peer, slot):
    return pltpu.make_async_remote_copy(
        src_ref=src.at[peer],
        dst_ref=dst.at[slot],
        send_sem=send.at[peer],
        recv_sem=recv.at[slot],
        device_id={"dom": peer},
        device_id_type=MESH,
    )


def each_dom(me, act):
    def one(i, carry):
        act(lax.rem(me + i, N_DOM))
        return carry

    lax.fori_loop(1, N_DOM, one, 0)


def build_lists(lists_ref, counts_ref, first_list, tiles, pieces, put):
    highs = tiles.shape[0]
    for c in range(4):
        for p, part in enumerate(thirds(tiles[:, c, :].T)):
            pieces[p, 128 * c : 128 * (c + 1), :] = part

    def one_list(l, carry):
        index = lists_ref[pl.ds(first_list + l, 1), :]
        high = lax.shift_right_logical(index, 7)
        low = jnp.bitwise_and(index, 127)
        pick = lax.broadcasted_iota(jnp.int32, (highs, LIST), 0) == high
        pick = jnp.where(pick, 1.0, 0.0).astype(BF16)
        rows = jnp.zeros((512, LIST), F32)
        for p in range(3):
            rows = rows + jnp.dot(pieces[p], pick, preferred_element_type=F32)
        here = lax.broadcasted_iota(jnp.int32, (128, LIST), 0) == low
        valid = lax.broadcasted_iota(jnp.int32, (1, LIST), 1) < counts_ref[first_list + l]
        picked = [
            jnp.sum(jnp.where(here, rows[128 * c : 128 * (c + 1)], 0.0), axis=0, keepdims=True)
            for c in range(4)
        ]
        mass = jnp.where(valid, -0.25 * picked[3], 0.0)
        put(l, jnp.concatenate([0.5 * picked[0], 0.5 * picked[1], 0.5 * picked[2], mass], axis=0))
        return carry

    lax.fori_loop(0, SHARE, one_list, 0)


def forward_kernel(
    counts_ref,
    tt_ref,
    pos_ref,
    nodes_ref,
    lists_ref,
    table_ref,
    arr_ref,
    codes_ref,
    oh_ref,
    nrecv,
    tiles,
    pieces,
    csend,
    crecv,
    ssend,
    srecv,
    mid,
    arr,
    trecv,
    n_send,
    n_recv,
    c_send,
    c_recv,
    s_send,
    s_recv,
    t_send,
    t_recv,
    d_send,
    d_recv,
):
    me_dom = lax.axis_index("dom")
    me = lax.axis_index("sub")
    barrier = greet(me_dom, me)

    dom_ids = lax.broadcasted_iota(jnp.int32, (N_DOM, 128), 0)
    wants = [dom_ids == tt_ref[j : j + 1, :] for j in range(TOP)]
    ones_of = [jnp.where(w, 1.0, 0.0) for w in wants]
    csend[...] = (ones_of[0] + ones_of[1]) + (ones_of[2] + ones_of[3])
    pl.semaphore_wait(barrier, N_SUB - 1 + N_DOM - 1)
    start_sub(lambda peer: csend, crecv, c_send, c_recv, me)
    start_sub(lambda peer: nodes_ref, nrecv, n_send, n_recv, me)

    earlier = lax.broadcasted_iota(jnp.int32, (128, 128), 0) < lax.broadcasted_iota(
        jnp.int32, (128, 128), 1
    )
    earlier = jnp.where(earlier, 1.0, 0.0).astype(BF16)
    full = jnp.ones((128, 128), BF16)
    within = [jnp.dot(o.astype(BF16), earlier, preferred_element_type=F32) for o in ones_of]
    total = [jnp.dot(o.astype(BF16), full, preferred_element_type=F32) for o in ones_of]
    pos_parts = [thirds(pos_ref[:, c, :]) for c in range(3)]
    wait_sub_recv(lambda peer: csend, crecv, c_send, c_recv, me)
    before = jnp.zeros((N_DOM, 128), F32)
    for p in range(1, N_SUB):
        peer = lax.rem(me + p, N_SUB)
        before = before + jnp.where(peer < me, 1.0, 0.0) * crecv[peer]
    base = jnp.dot(before.astype(BF16), full, preferred_element_type=F32)
    sharer, turn = [], []
    for j in range(TOP):
        place = (base + within[j]).astype(jnp.int32)
        base = base + total[j]
        sharer.append(jnp.bitwise_and(place, N_SUB - 1))
        turn.append(lax.shift_right_logical(place, 3))
    for t in range(N_SUB):
        hot = jnp.zeros((N_DOM, 128), F32)
        code = jnp.zeros((N_DOM, 128), F32)
        for j in range(TOP):
            mine = wants[j] & (sharer[j] == t)
            hot = jnp.where(mine, 1.0, hot)
            mark = tt_ref[TOP + j : TOP + j + 1, :] + (1 + GROUPS * turn[j])
            code = jnp.where(mine, mark.astype(F32), code)
        oh_ref[N_DOM * t : N_DOM * (t + 1), :] = hot.astype(BF16)
        ssend[t, :, 768:896] = jnp.dot(code.astype(BF16), full, preferred_element_type=F32)
    picks = oh_ref[:, 0:BLK]
    for c in range(3):
        rows = jnp.zeros((N_SUB * N_DOM, 256), F32)
        for part in pos_parts[c]:
            rows = rows + jnp.dot(picks, part, preferred_element_type=F32)
        for t in range(N_SUB):
            ssend[t, :, 256 * c : 256 * (c + 1)] = rows[N_DOM * t : N_DOM * (t + 1)]
    start_sub(lambda peer: ssend.at[peer], srecv, s_send, s_recv, me)
    srecv[me] = ssend[me]

    nrecv[me] = nodes_ref[...]
    wait_sub_recv(lambda peer: nodes_ref, nrecv, n_send, n_recv, me)

    def owner_tiles(o, carry):
        for j in range(NODE_DEV // 128):
            tiles[o * (NODE_DEV // 128) + j] = nrecv[o, :, 128 * j : 128 * (j + 1)]
        return carry

    lax.fori_loop(0, N_SUB, owner_tiles, 0)

    def put(l, value):
        trecv[me, l] = value

    build_lists(lists_ref, counts_ref, me * SHARE, tiles, pieces, put)
    start_sub(lambda peer: trecv.at[me], trecv, t_send, t_recv, me)

    wait_sub_recv(lambda peer: ssend.at[peer], srecv, s_send, s_recv, me)
    for k in range(2):
        for q in range(7):
            value = jnp.zeros((N_DOM, 128), F32)
            for src in range(N_SUB):
                code = srecv[src, :, 768:896]
                mine = (code > GROUPS + 0.5) if k else ((code > 0.5) & (code < GROUPS + 0.5))
                if q == 6:
                    value = jnp.where(mine, code - float(GROUPS * k), value)
                else:
                    value = jnp.where(mine, srecv[src, :, 128 * q : 128 * (q + 1)], value)
            mid[:, k, q, :] = value
        mid[:, k, 7, :] = jnp.zeros((N_DOM, 128), F32)
    each_dom(me_dom, lambda peer: dom_copy(mid, arr, d_send, d_recv, peer, me_dom).start())
    arr[me_dom] = jnp.zeros((2, 8, 128), F32)
    for src in range(N_SUB):
        codes_ref[src] = srecv[src, :, 768:896]

    wait_sub_recv(lambda peer: trecv.at[me], trecv, t_send, t_recv, me)
    for src in range(N_SUB):
        table_ref[SHARE * src : SHARE * (src + 1)] = trecv[src]
    each_dom(me_dom, lambda peer: dom_copy(mid, arr, d_send, d_recv, peer, peer).wait_recv())
    for k in range(2):
        arr_ref[:, k] = arr[:, k]

    wait_sub_send(lambda peer: csend, crecv, c_send, c_recv, me)
    wait_sub_send(lambda peer: nodes_ref, nrecv, n_send, n_recv, me)
    wait_sub_send(lambda peer: ssend.at[peer], srecv, s_send, s_recv, me)
    wait_sub_send(lambda peer: trecv.at[me], trecv, t_send, t_recv, me)
    each_dom(me_dom, lambda peer: dom_copy(mid, arr, d_send, d_recv, peer, me_dom).wait_send())


def forward(counts, tt, pos, nodes, lists):
    vmem = pl.BlockSpec(memory_space=pltpu.VMEM)
    dma = pltpu.SemaphoreType.DMA
    return pl.pallas_call(
        forward_kernel,
        out_shape=(
            jax.ShapeDtypeStruct((GROUPS, 4, LIST), F32),
            jax.ShapeDtypeStruct((N_DOM, 2, 8, 128), F32),
            jax.ShapeDtypeStruct((N_SUB, N_DOM, 128), F32),
            jax.ShapeDtypeStruct((N_SUB * N_DOM, 128), BF16),
        ),
        in_specs=[pl.BlockSpec(memory_space=pltpu.SMEM)] + [vmem] * 4,
        out_specs=(vmem,) * 4,
        scratch_shapes=[
            pltpu.VMEM((N_SUB, 4, NODE_DEV), F32),
            pltpu.VMEM((N_SUB * NODE_DEV // 128, 4, 128), F32),
            pltpu.VMEM((3, 512, N_SUB * NODE_DEV // 128), BF16),
            pltpu.VMEM((N_DOM, 128), F32),
            pltpu.VMEM((N_SUB, N_DOM, 128), F32),
            pltpu.VMEM((N_SUB, N_DOM, 896), F32),
            pltpu.VMEM((N_SUB, N_DOM, 896), F32),
            pltpu.VMEM((N_DOM, 2, 8, 128), F32),
            pltpu.VMEM((N_DOM, 2, 8, 128), F32),
            pltpu.VMEM((N_SUB, SHARE, 4, LIST), F32),
        ]
        + [dma((N_SUB,))] * 8
        + [dma((N_DOM,))] * 2,
        compiler_params=pltpu.CompilerParams(
            collective_id=0, has_side_effects=True, vmem_limit_bytes=48 * 2**20
        ),
    )(counts, tt, pos, nodes, lists)


def pair_sums(xs, node, acc):
    out = list(acc)
    for g in range(CHUNK // 8):
        rows = slice(8 * g, 8 * g + 8)
        cols = [jnp.concatenate([node[c][rows]] * 2, axis=1) for c in range(4)]
        d = [xs[c] - cols[c] for c in range(3)]
        s = d[0] * d[0] + (d[1] * d[1] + (d[2] * d[2] + 0.01))
        inv = lax.rsqrt(s)
        e = jnp.exp2(s * (-LOG2E))
        tail = 1.0 - lax.erf(s * inv)
        w = (inv * tail + SLOPE * e) * (inv * inv) * cols[3]
        out = [out[c] + d[c] * w for c in range(3)]
    return tuple(out)


def turn_tables(table_ref, cols):
    def one(l, carry):
        t = table_ref[l]
        t = jnp.concatenate([t, t], axis=0)
        cols[l, :, 0:8] = t.T
        return carry

    lax.fori_loop(0, GROUPS, one, 0, unroll=8)


def fetch(cols, row, i):
    n = cols[row, CHUNK * i : CHUNK * (i + 1), 0:8]
    return tuple(jnp.broadcast_to(n[:, c : c + 1], (CHUNK, 128)) for c in range(4))


def halves(rows):
    return [
        jnp.concatenate([jnp.broadcast_to(rows[2 * c + h], (8, 128)) for h in range(2)], axis=1)
        for c in range(3)
    ]


def import_kernel(rows_ref, counts_ref, arr_ref, table_ref, out_ref, cols, first):
    visits = rows_ref.shape[0]
    turn_tables(table_ref, cols)

    def prefetch(v):
        row = jnp.maximum(rows_ref[v], 0)
        for c, col in enumerate(fetch(cols, row, 0)):
            first[c] = col

    prefetch(0)

    def visit(v, carry):
        row = rows_ref[v]
        nxt = jnp.minimum(v + 1, visits - 1)
        safe = jnp.maximum(row, 0)
        steps = (counts_ref[safe] + (CHUNK - 1)) // CHUNK
        index = jnp.where(
            row < 0, 0, jnp.clip(steps - (MIN_STEPS - 1), 1, LIST // CHUNK - MIN_STEPS + 1)
        )

        def dead():
            prefetch(nxt)
            out_ref[v] = jnp.zeros((8, 128), F32)

        def alive(n):
            def run():
                x = arr_ref[v] * 0.5
                xs = halves([x[q : q + 1] for q in range(6)])
                zero = jnp.zeros((8, 256), F32)
                acc = pair_sums(xs, tuple(first[c] for c in range(4)), (zero, zero, zero))
                prefetch(nxt)
                for i in range(1, n):
                    acc = pair_sums(xs, fetch(cols, safe, i), acc)
                sums = [jnp.sum(a, axis=0, keepdims=True) for a in acc]
                rows = [sums[c][:, 128 * h : 128 * (h + 1)] for c in range(3) for h in range(2)]
                out_ref[v] = jnp.concatenate(rows + [jnp.zeros((2, 128), F32)], axis=0)

            return run

        lax.switch(index, [dead] + [alive(n) for n in range(MIN_STEPS, LIST // CHUNK + 1)])
        return carry

    lax.fori_loop(0, visits, visit, 0)


def import_pulls(rows, counts, arrived, table):
    smem = pl.BlockSpec(memory_space=pltpu.SMEM)
    vmem = pl.BlockSpec(memory_space=pltpu.VMEM)
    return pl.pallas_call(
        import_kernel,
        out_shape=jax.ShapeDtypeStruct(arrived.shape, F32),
        in_specs=[smem, smem, vmem, vmem],
        out_specs=vmem,
        scratch_shapes=[pltpu.VMEM((GROUPS, LIST, 128), F32), pltpu.VMEM((4, CHUNK, 128), F32)],
        compiler_params=pltpu.CompilerParams(vmem_limit_bytes=48 * 2**20),
    )(rows, counts, arrived, table)


def return_kernel(
    groups_ref,
    pos_ref,
    bins_ref,
    table_ref,
    pulls_ref,
    codes_ref,
    oh_ref,
    out_ref,
    cols,
    first,
    home,
    ret,
    bsend,
    brecv,
    d_send,
    d_recv,
    b_send,
    b_recv,
):
    me_dom = lax.axis_index("dom")
    me = lax.axis_index("sub")
    barrier = greet(me_dom, me)
    turn_tables(table_ref, cols)
    ret[me_dom] = jnp.zeros((2, 8, 128), F32)
    pl.semaphore_wait(barrier, N_SUB - 1 + N_DOM - 1)
    each_dom(me_dom, lambda peer: dom_copy(pulls_ref, ret, d_send, d_recv, peer, me_dom).start())

    def prefetch(v):
        for c, col in enumerate(fetch(cols, groups_ref[v], 0)):
            first[c] = col

    def home_block(v, carry):
        x = pos_ref[v] * 0.5
        xs = [jnp.broadcast_to(x[c : c + 1], (8, 256)) for c in range(3)]
        zero = jnp.zeros((8, 256), F32)
        acc = pair_sums(xs, tuple(first[c] for c in range(4)), (zero, zero, zero))
        prefetch(jnp.minimum(v + 1, BLK - 1))
        for i in range(1, LIST // CHUNK):
            acc = pair_sums(xs, fetch(cols, groups_ref[v], i), acc)
        for c in range(3):
            home[c, pl.ds(v, 1), :] = jnp.sum(acc[c], axis=0, keepdims=True)
        return carry

    prefetch(0)
    lax.fori_loop(0, EARLY, home_block, 0)

    each_dom(me_dom, lambda peer: dom_copy(pulls_ref, ret, d_send, d_recv, peer, peer).wait_recv())
    for q in range(6):
        low, high = ret[:, 0, q, :], ret[:, 1, q, :]
        for t in range(N_SUB):
            code = codes_ref[t]
            value = jnp.where(code > GROUPS + 0.5, high, jnp.where(code > 0.5, low, 0.0))
            bsend[t, :, 128 * q : 128 * (q + 1)] = value
    start_sub(lambda peer: bsend.at[peer], brecv, b_send, b_recv, me)
    brecv[me] = bsend[me]

    lax.fori_loop(EARLY, BLK, home_block, 0)

    wait_sub_recv(lambda peer: bsend.at[peer], brecv, b_send, b_recv, me)
    active = jnp.where(bins_ref[...] <= CUR_BIN, 1.0, 0.0)
    picks = oh_ref[...]
    for c in range(3):
        back = jnp.concatenate([brecv[t, :, 256 * c : 256 * (c + 1)] for t in range(N_SUB)], axis=0)
        total = home[c]
        for part in thirds(back):
            got = lax.dot_general(
                picks, part, (((0,), (0,)), ((), ())), preferred_element_type=F32
            )
            total = total + got[0:BLK]
        out_ref[:, c, :] = total * active

    each_dom(me_dom, lambda peer: dom_copy(pulls_ref, ret, d_send, d_recv, peer, me_dom).wait_send())
    wait_sub_send(lambda peer: bsend.at[peer], brecv, b_send, b_recv, me)


EARLY = 24


def finish(groups, pos, bins, table, pulls, codes, oh):
    vmem = pl.BlockSpec(memory_space=pltpu.VMEM)
    dma = pltpu.SemaphoreType.DMA
    return pl.pallas_call(
        return_kernel,
        out_shape=jax.ShapeDtypeStruct((BLK, 3, 256), F32),
        in_specs=[pl.BlockSpec(memory_space=pltpu.SMEM)] + [vmem] * 6,
        out_specs=vmem,
        scratch_shapes=[
            pltpu.VMEM((GROUPS, LIST, 128), F32),
            pltpu.VMEM((4, CHUNK, 128), F32),
            pltpu.VMEM((3, BLK, 256), F32),
            pltpu.VMEM((N_DOM, 2, 8, 128), F32),
            pltpu.VMEM((N_SUB, N_DOM, 768), F32),
            pltpu.VMEM((N_SUB, N_DOM, 768), F32),
            dma((N_DOM,)),
            dma((N_DOM,)),
            dma((N_SUB,)),
            dma((N_SUB,)),
        ],
        compiler_params=pltpu.CompilerParams(
            collective_id=1, has_side_effects=True, vmem_limit_bytes=48 * 2**20
        ),
    )(groups, pos, bins, table, pulls, codes, oh)


def local(
    positions,
    time_bins,
    home_groups,
    targets,
    target_groups,
    node_pos,
    node_mass,
    node_lists,
    list_counts,
):
    tt = jnp.pad(
        jnp.concatenate([targets, target_groups], axis=1).T,
        ((0, 0), (0, 128 - BLK)),
        constant_values=-1,
    )
    nodes = jnp.concatenate([node_pos, node_mass[None]], axis=0)
    table, arrived, codes, oh = forward(list_counts, tt, positions, nodes, node_lists)
    arrived = arrived.reshape(2 * N_DOM, 8, 128)
    rows = arrived[:, 6, 0].astype(jnp.int32) - 1
    pulls = import_pulls(rows, list_counts, arrived, table)
    return finish(
        home_groups, positions, time_bins, table, pulls.reshape(N_DOM, 2, 8, 128), codes, oh
    )


def solution(mesh):
    return jax.shard_map(
        local,
        mesh=mesh,
        in_specs=(
            P(("dom", "sub"), None, None),
            P(("dom", "sub"), None),
            P(("dom", "sub")),
            P(("dom", "sub"), None),
            P(("dom", "sub"), None),
            P(None, ("dom", "sub")),
            P(("dom", "sub")),
            P("dom", None),
            P("dom"),
        ),
        out_specs=P(("dom", "sub"), None, None),
        check_vma=False,
    )
```

time: 211 us -> 99.6 us (0.47)
  starting transfers between devices: 46.6 us -> 0 us
  Pallas kernels: 48.4 us -> 93.6 us
  waiting for transfers between devices: 33.4 us -> 0 us
  blocking collectives: 28.2 us -> 0 us
  other arithmetic: 27.2 us -> 2.82 us
  local copies, waits for them, and re-layouts: 24.6 us -> 2.48 us
    all_to_all x8 -> x0, starting transfers between devices: 46.6 us -> none  [the longest x2 14.4 us: local(): lax.all_to_all(a, 'dom', split_axis=0, concat_axis=0, tiled=True)]
    pallas_call x3, Pallas kernels: 48.4 us -> 93.6 us  [the longest x1 41.6 us: forward(): pl.pallas_call(forward_kernel, out_shape=(jax.ShapeDtypeStruct((GROUPS, 4...]
    all_to_all x8 -> x0, waiting for transfers between devices: 33.4 us -> none  [the longest x1 9.64 us: local(): lax.all_to_all(out_pos, 'sub', split_axis=0, concat_axis=0, tiled=True)]
    all_gather x2 -> x0, blocking collectives: 28.2 us -> none  [the longest x1 15.3 us: local(): lax.all_gather(jnp.concatenate([node_pos, node_mass[None]], axis=0), 'sub')]
    select_n x12 -> x0, other arithmetic: 22 us -> none  [the longest x1 20.1 us: local(): row_slot = row_place // sharers]
    gather x11 -> x0, local copies, waits for them, and re-layouts: 13.4 us -> none  [the longest x1 1.94 us: local(): pair_block[source_row]]
  transfers between devices with their start and end apart: 8 -> 0, of which waited for: 6 -> 0; matrix products, arithmetic and copies ran while one was open for 5% -> 0% of each run, Pallas kernels for 12% -> 0%
where the time goes in v2:
time: 99.6 us; the launch traced here: 99 us
  Pallas kernels  93.6 us (94%)
  other arithmetic  2.82 us (3%)
  local copies, waits for them, and re-layouts  2.48 us (2%)
    pallas_call x1, Pallas kernels, forward(): pl.pallas_call(forward_kernel, out_shape=(jax.ShapeDtypeStruct((GROUPS, 4...  41.6 us
    pallas_call x1, Pallas kernels, finish(): pl.pallas_call(return_kernel, out_shape=jax.ShapeDtypeStruct((BLK, 3, 256...  29.3 us
    pallas_call x1, Pallas kernels, import_pulls(): pl.pallas_call(import_kernel, out_shape=jax.ShapeDtypeStruct(arrived.shap...  22.7 us

profile of v2, /device:TPU:1, one launch (start us, length us, event | category | flops | bytes accessed | tf_op | source)
XLA Modules:
  0.0 99.0 jit_solution(6563634008912706913)
XLA Ops:
  0.0 0.0 copy-start.4
  0.0 0.7 add_bitcast_fusion
  0.7 0.0 copy-done.4
  0.7 0.9 pad_maximum_fusion.nodes_ref
  1.6 0.0 copy-start
  1.6 0.0 copy-start.2
  1.6 1.1 %copy.14.pos_ref = f32[64,3,256]{2,1,0:T(4,128)S(1)} copy(f32[64,3,256]{2,0,1:T(8,128)} %param.9) | data formatting | bytes 393216 | tf_op args[0]
  2.7 0.0 copy-done
  2.7 0.0 copy-done.2
  2.8 41.6 %shard_map.91 = (f32[64,4,256]{2,1,0:T(4,128)S(1)}, f32[32,2,8,128]{3,2,1,0:T(8,128)S(1)}, f32[8,32,128]{2,1,0:T(8,128)S(1)}, bf16[256,128]{1,0:T(8,128)(2,1)S(1)}) custom-call(s32[64]{0:T(128)S(1)} %copy-done.2, s32[8,128]{1,0:T(8,128)S(1)} %pad.4.tt_ref, f32[64,3,256]{2,1,0:T(4,128)S(1)} %copy.14.pos_ref, f32[4,4096]{1,0:T(4,128)S(1)} %pad_maximum_fusion.nodes_ref, ...), custom_call_target="tpu_custom_call" | custom-call | tf_op jit(solution)/shard_map/pallas_call | solution.py:262
  44.4 1.2 %fusion.1.rows_ref = s32[64]{0:T(128)S(1)} fusion(f32[64,8,128]{2,1,0:T(8,128)S(1)} %bitcast.6), kind=kLoop, calls=%fused_computation.3 | loop fusion | flops 128 | bytes 512 | tf_op jit(solution)/shard_map/sub | solution.py:511
  45.6 0.0 copy-start.1
  45.7 22.7 %shard_map.92 = f32[64,8,128]{2,1,0:T(8,128)S(1)} custom-call(s32[64]{0:T(128)S(1)} %fusion.1.rows_ref, s32[64]{0:T(128)S(1)} %copy-done.2, f32[64,8,128]{2,1,0:T(8,128)S(1)} %bitcast.7, f32[64,4,256]{2,1,0:T(4,128)S(1)} %get-tuple-element.9.table_ref), custom_call_target="tpu_custom_call" | custom-call | tf_op jit(solution)/shard_map/pallas_call | solution.py:377
  68.3 0.0 copy-start.3
  68.4 0.0 copy-done.1
  68.4 0.6 copy-done.3
  69.0 29.3 %shard_map.93 = f32[64,3,256]{2,1,0:T(4,128)S(1)} custom-call(s32[64]{0:T(128)S(1)} %copy-done.3, f32[64,3,256]{2,1,0:T(4,128)S(1)} %copy.14.pos_ref, s32[64,256]{1,0:T(8,128)S(1)} %copy-done.1, f32[64,4,256]{2,1,0:T(4,128)S(1)} %get-tuple-element.9.table_ref, f32[32,2,8,128]{3,2,1,0:T(8,128)S(1)} %bitcast.5, f32[8,32,128]{2,1,0:T(8,128)S(1)} %get-tuple-element.11.codes_ref, ...), custom_call_target="tpu_custom_call" | custom-call | tf_op jit(solution)/shard_map/pallas_call | solution.py:469
  98.3 0.7 copy.15
  (1 shorter events, 0.0 us)
Async XLA Ops:
  0.0 0.7 copy-start.4
  1.6 1.1 %copy-start = (s32[64,256]{1,0:T(8,128)S(1)}, s32[64,256]{1,0:T(8,128)}, u32[]{:S(2)}) copy-start(s32[64,256]{1,0:T(8,128)} %lists_ref.1) | copy-start | bytes 196612
  1.6 1.1 %copy-start.2 = (s32[64]{0:T(128)S(1)}, s32[64]{0:T(128)}, u32[]{:S(2)}) copy-start(s32[64]{0:T(128)} %counts_ref.3) | copy-start | bytes 772
  45.6 22.7 %copy-start.1 = (s32[64,256]{1,0:T(8,128)S(1)}, s32[64,256]{1,0:T(8,128)}, u32[]{:S(2)}) copy-start(s32[64,256]{1,0:T(8,128)} %bins_ref.1) | copy-start | bytes 196612
  68.3 0.7 copy-start.3

commit v3 on v2

v3 whole, which is shorter than its diff:
```python
import jax
import jax.numpy as jnp
from jax import lax
from jax.experimental import pallas as pl
from jax.experimental.pallas import tpu as pltpu
from jax.sharding import PartitionSpec as P

CUR_BIN = 2
LOG2E = 1.4426950408889634
SLOPE = 1.1283791670955126
GROUPS = 64
LIST = 256
N_DOM = 32
N_SUB = 8
TOP = 4
BLK = 64
NODE_DEV = 4096
FIRST = 8
SECOND = 28
SHARE = GROUPS // N_SUB
MESH = pl.DeviceIdType.MESH
F32 = jnp.float32
BF16 = jnp.bfloat16


def thirds(value):
    parts = []
    for _ in range(3):
        part = value.astype(BF16)
        parts.append(part)
        value = value - part.astype(F32)
    return parts


def greet(me_dom, me_sub):
    barrier = pltpu.get_barrier_semaphore()
    for p in range(1, N_SUB):
        pl.semaphore_signal(
            barrier, inc=1, device_id={"sub": lax.rem(me_sub + p, N_SUB)}, device_id_type=MESH
        )

    def one(i, carry):
        pl.semaphore_signal(
            barrier, inc=1, device_id={"dom": lax.rem(me_dom + i, N_DOM)}, device_id_type=MESH
        )
        return carry

    lax.fori_loop(1, N_DOM, one, 0)
    return barrier


def to_sub(src, dst, send, recv, peer, slot, mine):
    return pltpu.make_async_remote_copy(
        src_ref=src,
        dst_ref=dst.at[slot],
        send_sem=send.at[peer],
        recv_sem=recv.at[slot],
        device_id={"sub": peer},
        device_id_type=MESH,
    )


def start_sub(src_of, dst, send, recv, me):
    for p in range(1, N_SUB):
        peer = lax.rem(me + p, N_SUB)
        to_sub(src_of(peer), dst, send, recv, peer, me, me).start()


def wait_sub_recv(src_of, dst, send, recv, me):
    for p in range(1, N_SUB):
        peer = lax.rem(me + p, N_SUB)
        to_sub(src_of(peer), dst, send, recv, peer, peer, me).wait_recv()


def wait_sub_send(src_of, dst, send, recv, me):
    for p in range(1, N_SUB):
        peer = lax.rem(me + p, N_SUB)
        to_sub(src_of(peer), dst, send, recv, peer, me, me).wait_send()


def dom_copy(src, dst, send, recv, peer, slot):
    return pltpu.make_async_remote_copy(
        src_ref=src.at[peer],
        dst_ref=dst.at[slot],
        send_sem=send.at[peer],
        recv_sem=recv.at[slot],
        device_id={"dom": peer},
        device_id_type=MESH,
    )


def each_dom(me, act):
    def one(i, carry):
        act(lax.rem(me + i, N_DOM))
        return carry

    lax.fori_loop(1, N_DOM, one, 0)


def build_lists(lists_ref, counts_ref, first_list, tiles, pieces, put):
    highs = tiles.shape[0]
    for c in range(4):
        for p, part in enumerate(thirds(tiles[:, c, :].T)):
            pieces[p, 128 * c : 128 * (c + 1), :] = part

    def one_list(l, carry):
        index = lists_ref[pl.ds(first_list + l, 1), :]
        high = lax.shift_right_logical(index, 7)
        low = jnp.bitwise_and(index, 127)
        pick = lax.broadcasted_iota(jnp.int32, (highs, LIST), 0) == high
        pick = jnp.where(pick, 1.0, 0.0).astype(BF16)
        rows = jnp.zeros((512, LIST), F32)
        for p in range(3):
            rows = rows + jnp.dot(pieces[p], pick, preferred_element_type=F32)
        here = lax.broadcasted_iota(jnp.int32, (128, LIST), 0) == low
        valid = lax.broadcasted_iota(jnp.int32, (1, LIST), 1) < counts_ref[first_list + l]
        picked = [
            jnp.sum(jnp.where(here, rows[128 * c : 128 * (c + 1)], 0.0), axis=0, keepdims=True)
            for c in range(4)
        ]
        mass = jnp.where(valid, -0.25 * picked[3], 0.0)
        put(l, jnp.concatenate([0.5 * picked[0], 0.5 * picked[1], 0.5 * picked[2], mass], axis=0))
        return carry

    lax.fori_loop(0, SHARE, one_list, 0)


def back_copy(src, dst, k, send, recv, peer, slot):
    return pltpu.make_async_remote_copy(
        src_ref=src.at[k, peer],
        dst_ref=dst.at[slot, k],
        send_sem=send.at[peer],
        recv_sem=recv.at[slot],
        device_id={"dom": peer},
        device_id_type=MESH,
    )


def spread_tables(lists, wide):
    pick = lax.broadcasted_iota(jnp.int32, (8, 256), 0)
    side = jnp.where(lax.broadcasted_iota(jnp.int32, (8, 256), 1) < 128, 2, 5)
    pick = jnp.where((pick >= side) & (pick < side + 3), 1.0, 0.0).astype(BF16)

    def one(o, carry):
        for l in range(SHARE):
            t = lists[o, l]
            rows = [t[0:1], t[1:2]]
            for c in (2, 3):
                rows += [part.astype(F32) for part in thirds(t[c : c + 1])]
            t = jnp.concatenate(rows, axis=0).T
            for c in range(2):
                wide[o * SHARE + l, c] = jnp.broadcast_to(t[:, c : c + 1], (LIST, 128))
            both = jnp.dot(t.astype(BF16), pick, preferred_element_type=F32)
            for c in range(2):
                wide[o * SHARE + l, 2 + c] = both[:, 128 * c : 128 * (c + 1)]
        return carry

    lax.fori_loop(0, N_SUB, one, 0)


def visit_sums(wide, row, rows, held):
    sinks = [jnp.broadcast_to(r * 0.5, (8, 128)) for r in rows]
    acc = [jnp.zeros((8, 128), F32) for _ in range(6)]
    for g in range(LIST // 8):
        node = [wide[row, c, 8 * g : 8 * (g + 1), :] for c in range(4)]
        for h in range(2):
            d = [sinks[2 * c + h] - node[c] for c in range(3)]
            s = d[0] * d[0] + (d[1] * d[1] + (d[2] * d[2] + 0.01))
            inv = lax.rsqrt(s)
            e = jnp.exp2(s * (-LOG2E))
            tail = 1.0 - lax.erf(s * inv)
            w = (inv * tail + SLOPE * e) * (inv * inv) * node[3]
            for c in range(3):
                acc[2 * c + h] = acc[2 * c + h] + d[c] * w
    for q in range(6):
        held[q] = acc[q]


def whole_kernel(
    counts_ref,
    groups_ref,
    tt_ref,
    pos_ref,
    nodes_ref,
    lists_ref,
    bins_ref,
    out_ref,
    nrecv,
    tiles,
    pieces,
    csend,
    crecv,
    ssend,
    srecv,
    mid,
    arr,
    trecv,
    hots,
    wide,
    held,
    home,
    pulls,
    ret,
    bsend,
    brecv,
    picked_rows,
    rows_ref,
    rows_sem,
    n_send,
    n_recv,
    c_send,
    c_recv,
    s_send,
    s_recv,
    t_send,
    t_recv,
    b_send,
    b_recv,
    d_send,
    d_recv,
    low_send,
    low_recv,
    high_send,
    high_recv,
):
    me_dom = lax.axis_index("dom")
    me = lax.axis_index("sub")
    barrier = greet(me_dom, me)

    dom_ids = lax.broadcasted_iota(jnp.int32, (N_DOM, 128), 0)
    wants = [dom_ids == tt_ref[j : j + 1, :] for j in range(TOP)]
    ones_of = [jnp.where(w, 1.0, 0.0) for w in wants]
    csend[...] = (ones_of[0] + ones_of[1]) + (ones_of[2] + ones_of[3])
    earlier = lax.broadcasted_iota(jnp.int32, (128, 128), 0) < lax.broadcasted_iota(
        jnp.int32, (128, 128), 1
    )
    earlier = jnp.where(earlier, 1.0, 0.0).astype(BF16)
    full = jnp.ones((128, 128), BF16)
    within = [jnp.dot(o.astype(BF16), earlier, preferred_element_type=F32) for o in ones_of]
    total = [jnp.dot(o.astype(BF16), full, preferred_element_type=F32) for o in ones_of]
    pos_parts = [thirds(pos_ref[c]) for c in range(3)]
    held[...] = jnp.zeros((6, 8, 128), F32)
    pl.semaphore_wait(barrier, N_SUB - 1 + N_DOM - 1)
    start_sub(lambda peer: csend, crecv, c_send, c_recv, me)
    start_sub(lambda peer: nodes_ref, nrecv, n_send, n_recv, me)
    wait_sub_recv(lambda peer: csend, crecv, c_send, c_recv, me)
    before = jnp.zeros((N_DOM, 128), F32)
    for p in range(1, N_SUB):
        peer = lax.rem(me + p, N_SUB)
        before = before + jnp.where(peer < me, 1.0, 0.0) * crecv[peer]
    base = jnp.dot(before.astype(BF16), full, preferred_element_type=F32)
    sharer, turn = [], []
    for j in range(TOP):
        place = (base + within[j]).astype(jnp.int32)
        base = base + total[j]
        sharer.append(jnp.bitwise_and(place, N_SUB - 1))
        turn.append(lax.shift_right_logical(place, 3))
    for t in range(N_SUB):
        hot = jnp.zeros((N_DOM, 128), F32)
        code = jnp.zeros((N_DOM, 128), F32)
        for j in range(TOP):
            mine = wants[j] & (sharer[j] == t)
            hot = jnp.where(mine, 1.0, hot)
            mark = tt_ref[TOP + j : TOP + j + 1, :] + (1 + GROUPS * turn[j])
            code = jnp.where(mine, mark.astype(F32), code)
        hots[N_DOM * t : N_DOM * (t + 1), :] = hot.astype(BF16)
        ssend[t, :, 768:896] = jnp.dot(code.astype(BF16), full, preferred_element_type=F32)
    picks = hots[:, 0:BLK]
    for c in range(3):
        rows = jnp.zeros((N_SUB * N_DOM, 256), F32)
        for part in pos_parts[c]:
            rows = rows + jnp.dot(picks, part, preferred_element_type=F32)
        for t in range(N_SUB):
            ssend[t, :, 256 * c : 256 * (c + 1)] = rows[N_DOM * t : N_DOM * (t + 1)]
    start_sub(lambda peer: ssend.at[peer], srecv, s_send, s_recv, me)
    srecv[me] = ssend[me]

    nrecv[me] = nodes_ref[...]
    wait_sub_recv(lambda peer: nodes_ref, nrecv, n_send, n_recv, me)

    def owner_tiles(o, carry):
        for j in range(NODE_DEV // 128):
            tiles[o * (NODE_DEV // 128) + j] = nrecv[o, :, 128 * j : 128 * (j + 1)]
        return carry

    lax.fori_loop(0, N_SUB, owner_tiles, 0)

    def put(l, value):
        trecv[me, l] = value

    build_lists(lists_ref, counts_ref, me * SHARE, tiles, pieces, put)
    start_sub(lambda peer: trecv.at[me], trecv, t_send, t_recv, me)

    wait_sub_recv(lambda peer: ssend.at[peer], srecv, s_send, s_recv, me)
    for k in range(2):
        for q in range(7):
            value = jnp.zeros((N_DOM, 128), F32)
            for src in range(N_SUB):
                code = srecv[src, :, 768:896]
                mine = (code > GROUPS + 0.5) if k else ((code > 0.5) & (code < GROUPS + 0.5))
                if q == 6:
                    value = jnp.where(mine, code - float(GROUPS * k), value)
                else:
                    value = jnp.where(mine, srecv[src, :, 128 * q : 128 * (q + 1)], value)
            mid[:, k, q, :] = value
        mid[:, k, 7, :] = jnp.zeros((N_DOM, 128), F32)
    each_dom(me_dom, lambda peer: dom_copy(mid, arr, d_send, d_recv, peer, me_dom).start())
    arr[me_dom] = jnp.zeros((2, 8, 128), F32)
    ret[me_dom] = jnp.zeros((2, 8, 128), F32)

    wait_sub_recv(lambda peer: trecv.at[me], trecv, t_send, t_recv, me)
    spread_tables(trecv, wide)

    def home_rows(v):
        rows = [pos_ref[c, pl.ds(v, 1), :] for c in range(3)]
        return [r[:, 128 * h : 128 * (h + 1)] for r in rows for h in range(2)]

    def home_flush(v):
        for c in range(3):
            parts = [jnp.sum(held[2 * c + h], axis=0, keepdims=True) for h in range(2)]
            home[c, pl.ds(v, 1), :] = jnp.concatenate(parts, axis=1)

    def home_blocks(low, high):
        def one(v, carry):
            home_flush(jnp.maximum(v - 1, low))
            visit_sums(wide, groups_ref[v], home_rows(v), held)
            return carry

        lax.fori_loop(low, high, one, 0)
        home_flush(high - 1)

    home_blocks(0, FIRST)
    each_dom(me_dom, lambda peer: dom_copy(mid, arr, d_send, d_recv, peer, peer).wait_recv())
    diagonal = dom_ids == lax.broadcasted_iota(jnp.int32, (N_DOM, 128), 1)
    marks = [
        jnp.sum(jnp.where(diagonal, arr[:, k, 6, :], 0.0), axis=0, keepdims=True) for k in range(2)
    ]
    marks = jnp.concatenate(marks + [jnp.zeros((6, 128), F32)], axis=0)
    picked_rows[...] = jnp.clip(marks.astype(jnp.int32) - 1, 0, GROUPS - 1)
    to_scalars = pltpu.make_async_copy(picked_rows, rows_ref, rows_sem)
    to_scalars.start()
    to_scalars.wait()

    def imports(k, send, recv):
        def flush(i):
            rows = [jnp.sum(held[q], axis=0, keepdims=True) for q in range(6)]
            rows.append(jnp.zeros((2, 128), F32))
            pulls[k, lax.rem(me_dom + i, N_DOM)] = jnp.concatenate(rows, axis=0)

        def one(i, carry):
            flush(jnp.maximum(i - 1, 1))
            peer = lax.rem(me_dom + i, N_DOM)
            row = rows_ref[k, peer]
            visit_sums(wide, row, [arr[peer, k, q : q + 1, :] for q in range(6)], held)
            return carry

        lax.fori_loop(1, N_DOM, one, 0)
        flush(N_DOM - 1)
        each_dom(me_dom, lambda peer: back_copy(pulls, ret, k, send, recv, peer, me_dom).start())

    imports(0, low_send, low_recv)
    imports(1, high_send, high_recv)

    home_blocks(FIRST, SECOND)

    for k, send, recv in ((0, low_send, low_recv), (1, high_send, high_recv)):
        each_dom(me_dom, lambda peer: back_copy(pulls, ret, k, send, recv, peer, peer).wait_recv())
    for q in range(6):
        low, high = ret[:, 0, q, :], ret[:, 1, q, :]
        for t in range(N_SUB):
            code = srecv[t, :, 768:896]
            value = jnp.where(code > GROUPS + 0.5, high, jnp.where(code > 0.5, low, 0.0))
            bsend[t, :, 128 * q : 128 * (q + 1)] = value
    start_sub(lambda peer: bsend.at[peer], brecv, b_send, b_recv, me)
    brecv[me] = bsend[me]

    home_blocks(SECOND, BLK)

    wait_sub_recv(lambda peer: bsend.at[peer], brecv, b_send, b_recv, me)
    active = jnp.where(bins_ref[...] <= CUR_BIN, 1.0, 0.0)
    picks = hots[...]
    for c in range(3):
        back = jnp.concatenate([brecv[t, :, 256 * c : 256 * (c + 1)] for t in range(N_SUB)], axis=0)
        total = home[c]
        for part in thirds(back):
            got = lax.dot_general(
                picks, part, (((0,), (0,)), ((), ())), preferred_element_type=F32
            )
            total = total + got[0:BLK]
        out_ref[c] = total * active

    wait_sub_send(lambda peer: csend, crecv, c_send, c_recv, me)
    wait_sub_send(lambda peer: nodes_ref, nrecv, n_send, n_recv, me)
    wait_sub_send(lambda peer: ssend.at[peer], srecv, s_send, s_recv, me)
    wait_sub_send(lambda peer: trecv.at[me], trecv, t_send, t_recv, me)
    wait_sub_send(lambda peer: bsend.at[peer], brecv, b_send, b_recv, me)
    each_dom(me_dom, lambda peer: dom_copy(mid, arr, d_send, d_recv, peer, me_dom).wait_send())
    for k, send, recv in ((0, low_send, low_recv), (1, high_send, high_recv)):
        each_dom(me_dom, lambda peer: back_copy(pulls, ret, k, send, recv, peer, me_dom).wait_send())


def whole(counts, groups, tt, pos, nodes, lists, bins):
    smem = pl.BlockSpec(memory_space=pltpu.SMEM)
    vmem = pl.BlockSpec(memory_space=pltpu.VMEM)
    dma = pltpu.SemaphoreType.DMA
    return pl.pallas_call(
        whole_kernel,
        out_shape=jax.ShapeDtypeStruct((3, BLK, 256), F32),
        in_specs=[smem] * 2 + [vmem] * 5,
        out_specs=vmem,
        scratch_shapes=[
            pltpu.VMEM((N_SUB, 4, NODE_DEV), F32),
            pltpu.VMEM((N_SUB * NODE_DEV // 128, 4, 128), F32),
            pltpu.VMEM((3, 512, N_SUB * NODE_DEV // 128), BF16),
            pltpu.VMEM((N_DOM, 128), F32),
            pltpu.VMEM((N_SUB, N_DOM, 128), F32),
            pltpu.VMEM((N_SUB, N_DOM, 896), F32),
            pltpu.VMEM((N_SUB, N_DOM, 896), F32),
            pltpu.VMEM((N_DOM, 2, 8, 128), F32),
            pltpu.VMEM((N_DOM, 2, 8, 128), F32),
            pltpu.VMEM((N_SUB, SHARE, 4, LIST), F32),
            pltpu.VMEM((N_SUB * N_DOM, 128), BF16),
            pltpu.VMEM((GROUPS, 4, LIST, 128), F32),
            pltpu.VMEM((6, 8, 128), F32),
            pltpu.VMEM((3, BLK, 256), F32),
            pltpu.VMEM((2, N_DOM, 8, 128), F32),
            pltpu.VMEM((N_DOM, 2, 8, 128), F32),
            pltpu.VMEM((N_SUB, N_DOM, 768), F32),
            pltpu.VMEM((N_SUB, N_DOM, 768), F32),
            pltpu.VMEM((8, 128), jnp.int32),
            pltpu.SMEM((8, 128), jnp.int32),
            dma,
        ]
        + [dma((N_SUB,))] * 10
        + [dma((N_DOM,))] * 6,
        compiler_params=pltpu.CompilerParams(
            collective_id=0, has_side_effects=True, vmem_limit_bytes=50 * 2**20
        ),
    )(counts, groups, tt, pos, nodes, lists, bins)


def local(
    positions,
    time_bins,
    home_groups,
    targets,
    target_groups,
    node_pos,
    node_mass,
    node_lists,
    list_counts,
):
    tt = jnp.pad(
        jnp.concatenate([targets, target_groups], axis=1).T,
        ((0, 0), (0, 128 - BLK)),
        constant_values=-1,
    )
    nodes = jnp.concatenate([node_pos, node_mass[None]], axis=0)
    pos = jnp.transpose(positions, (1, 0, 2))
    out = whole(list_counts, home_groups, tt, pos, nodes, node_lists, time_bins)
    return jnp.transpose(out, (1, 0, 2))


def solution(mesh):
    return jax.shard_map(
        local,
        mesh=mesh,
        in_specs=(
            P(("dom", "sub"), None, None),
            P(("dom", "sub"), None),
            P(("dom", "sub")),
            P(("dom", "sub"), None),
            P(("dom", "sub"), None),
            P(None, ("dom", "sub")),
            P(("dom", "sub")),
            P("dom", None),
            P("dom"),
        ),
        out_specs=P(("dom", "sub"), None, None),
        check_vma=False,
    )
```

time: 99.6 us -> 88 us (0.88)
  Pallas kernels: 93.6 us -> 84.4 us
  other arithmetic: 2.82 us -> 1.64 us
    pallas_call x3 -> x1, Pallas kernels: 93.6 us -> 84.4 us  [whole(): pl.pallas_call(whole_kernel, out_shape=jax.ShapeDtypeStruct((3, BLK, 256)...]
    sub x1 -> x0, other arithmetic: 1.23 us -> none  [local(): rows = arrived[:, 6, 0].astype(jnp.int32) - 1]
where the time goes in v3:
time: 88 us; the launch traced here: 87.8 us
  Pallas kernels  84.4 us (96%)
  local copies, waits for them, and re-layouts  1.64 us (2%)
  other arithmetic  1.64 us (2%)
    pallas_call x1, Pallas kernels, whole(): pl.pallas_call(whole_kernel, out_shape=jax.ShapeDtypeStruct((3, BLK, 256)...  84.4 us

profile of v3, /device:TPU:1, one launch (start us, length us, event | category | flops | bytes accessed | tf_op | source)
XLA Modules:
  0.0 87.8 jit_solution(5152742038740797376)
XLA Ops:
  0.0 0.0 copy-start.5
  0.0 0.7 add_bitcast_fusion
  0.7 0.0 copy-done.5
  0.7 0.0 copy-start.1
  0.8 0.0 copy-start.2
  0.8 0.0 copy-start.3
  0.8 0.0 copy-start.4
  0.8 0.9 %pad_maximum_fusion.nodes_ref = f32[4,4096]{1,0:T(4,128)S(1)} fusion(f32[1,4096]{1,0:T(1,128)S(1)} %bitcast.7, f32[3,4096]{1,0:T(4,128)} %param.14), kind=kLoop, calls=%fused_computation | loop fusion | flops 16384 | bytes 131072 | tf_op jit(solution)/shard_map/concatenate | solution.py:458
  1.7 0.0 copy-done.1
  1.7 0.0 copy-done.2
  1.7 0.0 copy-done.3
  1.7 0.0 copy-done.4
  1.7 0.0 copy-start
  1.8 0.9 %copy-done = f32[64,3,256]{2,0,1:T(8,128)S(1)} copy-done((f32[64,3,256]{2,0,1:T(8,128)S(1)}, f32[64,3,256]{2,0,1:T(8,128)}, u32[]{:S(2)}) %copy-start) | copy-done | bytes 196632
  2.7 84.4 %shard_map.91 = f32[3,64,256]{2,1,0:T(8,128)S(1)} custom-call(s32[64]{0:T(128)S(1)} %copy-done.3, s32[64]{0:T(128)S(1)} %copy-done.4, s32[8,128]{1,0:T(8,128)S(1)} %pad.4.tt_ref, f32[3,64,256]{2,1,0:T(8,128)S(1)} %bitcast.6, f32[4,4096]{1,0:T(4,128)S(1)} %pad_maximum_fusion.nodes_ref, s32[64,256]{1,0:T(8,128)S(1)} %copy-done.1, s32[64,256]{1,0:T(8,128)S(1)} %copy-done.2), custom_call_target="tpu_custom_call" | custom-call | tf_op jit(solution)/shard_map/pallas_call | solution.py:406
  87.1 0.7 copy.11
  (1 shorter events, 0.0 us)
Async XLA Ops:
  0.0 0.7 copy-start.5
  0.7 1.0 %copy-start.1 = (s32[64,256]{1,0:T(8,128)S(1)}, s32[64,256]{1,0:T(8,128)}, u32[]{:S(2)}) copy-start(s32[64,256]{1,0:T(8,128)} %lists_ref.1) | copy-start | bytes 196612
  0.8 1.0 %copy-start.2 = (s32[64,256]{1,0:T(8,128)S(1)}, s32[64,256]{1,0:T(8,128)}, u32[]{:S(2)}) copy-start(s32[64,256]{1,0:T(8,128)} %bins_ref.1) | copy-start | bytes 196612
  0.8 1.0 %copy-start.3 = (s32[64]{0:T(128)S(1)}, s32[64]{0:T(128)}, u32[]{:S(2)}) copy-start(s32[64]{0:T(128)} %counts_ref.1) | copy-start | bytes 772
  0.8 1.0 %copy-start.4 = (s32[64]{0:T(128)S(1)}, s32[64]{0:T(128)}, u32[]{:S(2)}) copy-start(s32[64]{0:T(128)} %groups_ref.1) | copy-start | bytes 772
  1.7 0.9 %copy-start = (f32[64,3,256]{2,0,1:T(8,128)S(1)}, f32[64,3,256]{2,0,1:T(8,128)}, u32[]{:S(2)}) copy-start(f32[64,3,256]{2,0,1:T(8,128)} %param.9) | copy-start | bytes 589828

commit v4 on v3

--- a/solution.py
+++ b/solution.py
@@ -1,3 +1,4 @@
+import functools
 import jax
 import jax.numpy as jnp
 from jax import lax
@@ -15,8 +16,8 @@
 TOP = 4
 BLK = 64
 NODE_DEV = 4096
-FIRST = 8
-SECOND = 28
+FIRST = 2
+SECOND = 30
 SHARE = GROUPS // N_SUB
 MESH = pl.DeviceIdType.MESH
 F32 = jnp.float32
@@ -95,6 +96,81 @@
         return carry
 
     lax.fori_loop(1, N_DOM, one, 0)
+
+
+def ring_of(me):
+    x, core = me // 2, lax.rem(me, 2)
+    right = lax.rem(x + 1, N_SUB // 2) * 2 + core
+    left = lax.rem(x + 3, N_SUB // 2) * 2 + core
+    across = lax.rem(x + 2, N_SUB // 2) * 2 + core
+    return me, right, left, across, me + 1 - 2 * core
+
+
+def other(slot):
+    return slot + 1 - 2 * lax.rem(slot, 2)
+
+
+def ring_copies(own, whole, half, send, recv, ring):
+    me, right, left, across, pair = ring
+
+    def one(index, src, dst, sem, dev):
+        return pltpu.make_async_remote_copy(
+            src_ref=src,
+            dst_ref=dst,
+            send_sem=send.at[index],
+            recv_sem=recv.at[sem],
+            device_id={"sub": dev},
+            device_id_type=MESH,
+        )
+
+    return [
+        one(0, own, whole(me), me, right),
+        one(1, own, whole(me), me, left),
+        one(2, own, whole(me), me, pair),
+        one(3, half(left, 0), half(left, 0), N_SUB, right),
+        one(4, whole(left), whole(left), left, pair),
+        one(5, half(right, 1), half(right, 1), N_SUB + 1, left),
+        one(6, whole(right), whole(right), right, pair),
+        one(7, whole(across), whole(across), across, pair),
+    ]
+
+
+def ring_wait(whole, half, send, recv, ring, slot, part=None):
+    src = whole(slot) if part is None else half(slot, part)
+    pltpu.make_async_remote_copy(
+        src_ref=src,
+        dst_ref=src,
+        send_sem=send.at[0],
+        recv_sem=recv.at[slot if part is None else N_SUB + part],
+        device_id={"sub": ring[4]},
+        device_id_type=MESH,
+    ).wait_recv()
+
+
+def ring_one(copies):
+    for i in range(3):
+        copies[i].start()
+
+
+def ring_two(copies, wait, ring):
+    wait(ring[2])
+    copies[3].start()
+    copies[4].start()
+    wait(ring[1])
+    copies[5].start()
+    copies[6].start()
+
+
+def ring_three(copies, wait, ring):
+    wait(ring[3], 0)
+    wait(ring[3], 1)
+    copies[7].start()
+
+
+def ring_end(wait, ring):
+    wait(ring[4])
+    for slot in ring[1:4]:
+        wait(other(slot))
 
 
 def build_lists(lists_ref, counts_ref, first_list, tiles, pieces, put):
@@ -188,10 +264,11 @@
     nrecv,
     tiles,
     pieces,
-    csend,
     crecv,
-    ssend,
-    srecv,
+    precv,
+    places,
+    chosen,
+    codes,
     mid,
     arr,
     trecv,
@@ -210,8 +287,8 @@
     n_recv,
     c_send,
     c_recv,
-    s_send,
-    s_recv,
+    p_send,
+    p_recv,
     t_send,
     t_recv,
     b_send,
@@ -227,56 +304,94 @@
     me = lax.axis_index("sub")
     barrier = greet(me_dom, me)
 
+    ring = ring_of(me)
     dom_ids = lax.broadcasted_iota(jnp.int32, (N_DOM, 128), 0)
-    wants = [dom_ids == tt_ref[j : j + 1, :] for j in range(TOP)]
-    ones_of = [jnp.where(w, 1.0, 0.0) for w in wants]
-    csend[...] = (ones_of[0] + ones_of[1]) + (ones_of[2] + ones_of[3])
-    earlier = lax.broadcasted_iota(jnp.int32, (128, 128), 0) < lax.broadcasted_iota(
-        jnp.int32, (128, 128), 1
-    )
-    earlier = jnp.where(earlier, 1.0, 0.0).astype(BF16)
+    lanes = lax.broadcasted_iota(jnp.int32, (N_DOM, 128), 1)
+    row_ids = lax.broadcasted_iota(jnp.int32, (128, 128), 0)
+    col_ids = lax.broadcasted_iota(jnp.int32, (128, 128), 1)
+
+    def pattern(mask):
+        return jnp.where(mask, 1.0, 0.0).astype(BF16)
+
+    def count(value, matrix):
+        return jnp.dot(value.astype(BF16), matrix, preferred_element_type=F32)
+
+    same = (row_ids < BLK) == (col_ids < BLK)
+    earlier = pattern(same & (row_ids < col_ids))
+    block = pattern(same)
+    crossed = pattern((row_ids < BLK) & (col_ids >= BLK))
+    evens, odds = pattern(row_ids < BLK), pattern(row_ids >= BLK)
     full = jnp.ones((128, 128), BF16)
-    within = [jnp.dot(o.astype(BF16), earlier, preferred_element_type=F32) for o in ones_of]
-    total = [jnp.dot(o.astype(BF16), full, preferred_element_type=F32) for o in ones_of]
-    pos_parts = [thirds(pos_ref[c]) for c in range(3)]
     held[...] = jnp.zeros((6, 8, 128), F32)
+
+    def n_half(slot, h):
+        return nrecv.at[slot, :, pl.ds(NODE_DEV // 2 * h, NODE_DEV // 2)]
+
+    def p_half(slot, h):
+        return precv.at[slot, :, pl.ds(BLK // 2 * h, BLK // 2)]
+
+    n_whole, p_whole = nrecv.at.__getitem__, precv.at.__getitem__
+    n_copies = ring_copies(nodes_ref, n_whole, n_half, n_send, n_recv, ring)
+    p_copies = ring_copies(pos_ref, p_whole, p_half, p_send, p_recv, ring)
+    n_wait = functools.partial(ring_wait, n_whole, n_half, n_send, n_recv, ring)
+    p_wait = functools.partial(ring_wait, p_whole, p_half, p_send, p_recv, ring)
+
     pl.semaphore_wait(barrier, N_SUB - 1 + N_DOM - 1)
-    start_sub(lambda peer: csend, crecv, c_send, c_recv, me)
-    start_sub(lambda peer: nodes_ref, nrecv, n_send, n_recv, me)
-    wait_sub_recv(lambda peer: csend, crecv, c_send, c_recv, me)
-    before = jnp.zeros((N_DOM, 128), F32)
-    for p in range(1, N_SUB):
-        peer = lax.rem(me + p, N_SUB)
-        before = before + jnp.where(peer < me, 1.0, 0.0) * crecv[peer]
-    base = jnp.dot(before.astype(BF16), full, preferred_element_type=F32)
-    sharer, turn = [], []
-    for j in range(TOP):
-        place = (base + within[j]).astype(jnp.int32)
-        base = base + total[j]
-        sharer.append(jnp.bitwise_and(place, N_SUB - 1))
-        turn.append(lax.shift_right_logical(place, 3))
+    start_sub(lambda peer: tt_ref, crecv, c_send, c_recv, me)
+    ring_one(n_copies)
+    ring_one(p_copies)
+    crecv[me] = tt_ref[...]
+    nrecv[me] = nodes_ref[...]
+    precv[me] = pos_ref[...]
+    wait_sub_recv(lambda peer: tt_ref, crecv, c_send, c_recv, me)
+
+    base = jnp.zeros((N_DOM, 128), F32)
+    marks = [jnp.zeros((N_DOM, 128), F32) for _ in range(2)]
+    for pair in range(N_SUB // 2):
+        goal = jnp.where(lanes[0:8] < BLK, crecv[2 * pair], crecv[2 * pair + 1])
+        wants = [dom_ids == goal[j : j + 1, :] for j in range(TOP)]
+        ones_of = [jnp.where(w, 1.0, 0.0) for w in wants]
+        stack = jnp.concatenate(ones_of, axis=0)
+        within, block_total = count(stack, earlier), count(stack, block)
+        summed = (ones_of[0] + ones_of[1]) + (ones_of[2] + ones_of[3])
+        start = base + count(summed, crossed)
+        base = base + count(summed, full)
+        hot = [jnp.zeros((N_DOM, 128), F32) for _ in range(2)]
+        for j in range(TOP):
+            part = slice(N_DOM * j, N_DOM * (j + 1))
+            place = (start + within[part]).astype(jnp.int32)
+            start = start + block_total[part]
+            places[pair, j] = place
+            group = (goal[TOP + j : TOP + j + 1, :] + 1).astype(F32)
+            for k in range(2):
+                mine = wants[j] & (place == me + N_SUB * k)
+                hot[k] = jnp.where(mine, 1.0, hot[k])
+                marks[k] = marks[k] + jnp.where(mine, group, 0.0)
+        for k in range(2):
+            chosen[pair // 2, N_DOM * k : N_DOM * (k + 1), 128 * (pair % 2) : 128 * (pair % 2 + 1)] = (
+                hot[k].astype(BF16)
+            )
+        kinds = hot[0] + 2.0 * hot[1]
+        codes[2 * pair] = count(kinds, evens)
+        codes[2 * pair + 1] = count(kinds, odds)
+    ring_two(n_copies, n_wait, ring)
+    own_pair = me // 2
+    goal = jnp.where(lanes[0:8] < BLK, crecv[2 * own_pair], crecv[2 * own_pair + 1])
     for t in range(N_SUB):
         hot = jnp.zeros((N_DOM, 128), F32)
-        code = jnp.zeros((N_DOM, 128), F32)
         for j in range(TOP):
-            mine = wants[j] & (sharer[j] == t)
+            mine = (dom_ids == goal[j : j + 1, :]) & (
+                jnp.bitwise_and(places[own_pair, j], N_SUB - 1) == t
+            )
             hot = jnp.where(mine, 1.0, hot)
-            mark = tt_ref[TOP + j : TOP + j + 1, :] + (1 + GROUPS * turn[j])
-            code = jnp.where(mine, mark.astype(F32), code)
         hots[N_DOM * t : N_DOM * (t + 1), :] = hot.astype(BF16)
-        ssend[t, :, 768:896] = jnp.dot(code.astype(BF16), full, preferred_element_type=F32)
-    picks = hots[:, 0:BLK]
-    for c in range(3):
-        rows = jnp.zeros((N_SUB * N_DOM, 256), F32)
-        for part in pos_parts[c]:
-            rows = rows + jnp.dot(picks, part, preferred_element_type=F32)
-        for t in range(N_SUB):
-            ssend[t, :, 256 * c : 256 * (c + 1)] = rows[N_DOM * t : N_DOM * (t + 1)]
-    start_sub(lambda peer: ssend.at[peer], srecv, s_send, s_recv, me)
-    srecv[me] = ssend[me]
-
-    nrecv[me] = nodes_ref[...]
-    wait_sub_recv(lambda peer: nodes_ref, nrecv, n_send, n_recv, me)
+    for k in range(2):
+        mid[:, k, 6, :] = count(marks[k], full)
+        mid[:, k, 7, :] = jnp.zeros((N_DOM, 128), F32)
+    ring_two(p_copies, p_wait, ring)
+
+    ring_three(n_copies, n_wait, ring)
+    ring_end(n_wait, ring)
 
     def owner_tiles(o, carry):
         for j in range(NODE_DEV // 128):
@@ -290,20 +405,18 @@
 
     build_lists(lists_ref, counts_ref, me * SHARE, tiles, pieces, put)
     start_sub(lambda peer: trecv.at[me], trecv, t_send, t_recv, me)
-
-    wait_sub_recv(lambda peer: ssend.at[peer], srecv, s_send, s_recv, me)
-    for k in range(2):
-        for q in range(7):
-            value = jnp.zeros((N_DOM, 128), F32)
-            for src in range(N_SUB):
-                code = srecv[src, :, 768:896]
-                mine = (code > GROUPS + 0.5) if k else ((code > 0.5) & (code < GROUPS + 0.5))
-                if q == 6:
-                    value = jnp.where(mine, code - float(GROUPS * k), value)
-                else:
-                    value = jnp.where(mine, srecv[src, :, 128 * q : 128 * (q + 1)], value)
-            mid[:, k, q, :] = value
-        mid[:, k, 7, :] = jnp.zeros((N_DOM, 128), F32)
+    ring_three(p_copies, p_wait, ring)
+    ring_end(p_wait, ring)
+
+    for c in range(3):
+        rows = jnp.zeros((2 * N_DOM, 256), F32)
+        for h in range(2):
+            some = jnp.concatenate([precv[N_SUB // 2 * h + i, c] for i in range(N_SUB // 2)], axis=0)
+            for part in thirds(some):
+                rows = rows + jnp.dot(chosen[h], part, preferred_element_type=F32)
+        for k in range(2):
+            for h in range(2):
+                mid[:, k, 2 * c + h, :] = rows[N_DOM * k : N_DOM * (k + 1), 128 * h : 128 * (h + 1)]
     each_dom(me_dom, lambda peer: dom_copy(mid, arr, d_send, d_recv, peer, me_dom).start())
     arr[me_dom] = jnp.zeros((2, 8, 128), F32)
     ret[me_dom] = jnp.zeros((2, 8, 128), F32)
@@ -368,8 +481,8 @@
     for q in range(6):
         low, high = ret[:, 0, q, :], ret[:, 1, q, :]
         for t in range(N_SUB):
-            code = srecv[t, :, 768:896]
-            value = jnp.where(code > GROUPS + 0.5, high, jnp.where(code > 0.5, low, 0.0))
+            code = codes[t]
+            value = jnp.where(code > 1.5, high, jnp.where(code > 0.5, low, 0.0))
             bsend[t, :, 128 * q : 128 * (q + 1)] = value
     start_sub(lambda peer: bsend.at[peer], brecv, b_send, b_recv, me)
     brecv[me] = bsend[me]
@@ -386,12 +499,12 @@
             got = lax.dot_general(
                 picks, part, (((0,), (0,)), ((), ())), preferred_element_type=F32
             )
-            total = total + got[0:BLK]
+            total = total + jnp.where(lax.rem(me, 2) == 0, got[0:BLK], got[BLK : 2 * BLK])
         out_ref[c] = total * active
 
-    wait_sub_send(lambda peer: csend, crecv, c_send, c_recv, me)
-    wait_sub_send(lambda peer: nodes_ref, nrecv, n_send, n_recv, me)
-    wait_sub_send(lambda peer: ssend.at[peer], srecv, s_send, s_recv, me)
+    wait_sub_send(lambda peer: tt_ref, crecv, c_send, c_recv, me)
+    for copy in n_copies + p_copies:
+        copy.wait_send()
     wait_sub_send(lambda peer: trecv.at[me], trecv, t_send, t_recv, me)
     wait_sub_send(lambda peer: bsend.at[peer], brecv, b_send, b_recv, me)
     each_dom(me_dom, lambda peer: dom_copy(mid, arr, d_send, d_recv, peer, me_dom).wait_send())
@@ -412,10 +525,11 @@
             pltpu.VMEM((N_SUB, 4, NODE_DEV), F32),
             pltpu.VMEM((N_SUB * NODE_DEV // 128, 4, 128), F32),
             pltpu.VMEM((3, 512, N_SUB * NODE_DEV // 128), BF16),
-            pltpu.VMEM((N_DOM, 128), F32),
+            pltpu.VMEM((N_SUB, 8, 128), jnp.int32),
+            pltpu.VMEM((N_SUB, 3, BLK, 256), F32),
+            pltpu.VMEM((N_SUB // 2, TOP, N_DOM, 128), jnp.int32),
+            pltpu.VMEM((2, 2 * N_DOM, 256), BF16),
             pltpu.VMEM((N_SUB, N_DOM, 128), F32),
-            pltpu.VMEM((N_SUB, N_DOM, 896), F32),
-            pltpu.VMEM((N_SUB, N_DOM, 896), F32),
             pltpu.VMEM((N_DOM, 2, 8, 128), F32),
             pltpu.VMEM((N_DOM, 2, 8, 128), F32),
             pltpu.VMEM((N_SUB, SHARE, 4, LIST), F32),
@@ -431,7 +545,10 @@
             pltpu.SMEM((8, 128), jnp.int32),
             dma,
         ]
-        + [dma((N_SUB,))] * 10
+        + [dma((N_SUB,)), dma((N_SUB + 2,))]
+        + [dma((N_SUB,))] * 2
+        + [dma((N_SUB,)), dma((N_SUB + 2,))]
+        + [dma((N_SUB,))] * 4
         + [dma((N_DOM,))] * 6,
         compiler_params=pltpu.CompilerParams(
             collective_id=0, has_side_effects=True, vmem_limit_bytes=50 * 2**20
@@ -450,11 +567,8 @@
     node_lists,
     list_counts,
 ):
-    tt = jnp.pad(
-        jnp.concatenate([targets, target_groups], axis=1).T,
-        ((0, 0), (0, 128 - BLK)),
-        constant_values=-1,
-    )
+    tt = jnp.concatenate([targets, target_groups], axis=1).T
+    tt = jnp.concatenate([tt, tt], axis=1)
     nodes = jnp.concatenate([node_pos, node_mass[None]], axis=0)
     pos = jnp.transpose(positions, (1, 0, 2))
     out = whole(list_counts, home_groups, tt, pos, nodes, node_lists, time_bins)

time: 88 us -> 85.5 us (0.972)
  Pallas kernels: 84.4 us -> 81.9 us
    pallas_call x1, Pallas kernels: 84.4 us -> 81.9 us  [whole(): pl.pallas_call(whole_kernel, out_shape=jax.ShapeDtypeStruct((3, BLK, 256)...]
where the time goes in v4:
time: 85.5 us; the launch traced here: 85.3 us
  Pallas kernels  81.9 us (96%)
  other arithmetic  1.7 us (2%)
  local copies, waits for them, and re-layouts  1.62 us (2%)
    pallas_call x1, Pallas kernels, whole(): pl.pallas_call(whole_kernel, out_shape=jax.ShapeDtypeStruct((3, BLK, 256)...  81.9 us

profile of v4, /device:TPU:1, one launch (start us, length us, event | category | flops | bytes accessed | tf_op | source)
XLA Modules:
  0.0 85.3 jit_solution(2392664197407738301)
XLA Ops:
  0.0 0.0 copy-start.5
  0.0 0.7 add_bitcast_fusion
  0.7 0.1 pad_add_fusion.tt_ref
  0.8 0.0 copy-done.5
  0.8 0.0 copy-start.1
  0.8 0.0 copy-start.2
  0.8 0.0 copy-start.3
  0.8 0.0 copy-start.4
  0.8 0.9 %pad_maximum_fusion.nodes_ref = f32[4,4096]{1,0:T(4,128)S(1)} fusion(f32[1,4096]{1,0:T(1,128)S(1)} %bitcast.7, f32[3,4096]{1,0:T(4,128)} %param.14), kind=kLoop, calls=%fused_computation | loop fusion | flops 16384 | bytes 131072 | tf_op jit(solution)/shard_map/concatenate | solution.py:572
  1.7 0.0 copy-done.1
  1.7 0.0 copy-done.2
  1.8 0.0 copy-done.3
  1.8 0.0 copy-done.4
  1.8 0.0 copy-start
  1.8 0.9 %copy-done = f32[64,3,256]{2,0,1:T(8,128)S(1)} copy-done((f32[64,3,256]{2,0,1:T(8,128)S(1)}, f32[64,3,256]{2,0,1:T(8,128)}, u32[]{:S(2)}) %copy-start) | copy-done | bytes 196632
  2.7 81.9 %shard_map.91 = f32[3,64,256]{2,1,0:T(8,128)S(1)} custom-call(s32[64]{0:T(128)S(1)} %copy-done.3, s32[64]{0:T(128)S(1)} %copy-done.4, s32[8,128]{1,0:T(8,128)S(1)} %pad_add_fusion.tt_ref, f32[3,64,256]{2,1,0:T(8,128)S(1)} %bitcast.6, f32[4,4096]{1,0:T(4,128)S(1)} %pad_maximum_fusion.nodes_ref, s32[64,256]{1,0:T(8,128)S(1)} %copy-done.1, s32[64,256]{1,0:T(8,128)S(1)} %copy-done.2), custom_call_target="tpu_custom_call" | custom-call | tf_op jit(solution)/shard_map/pallas_call | solution.py:519
  84.6 0.7 copy.11
Async XLA Ops:
  0.0 0.8 copy-start.5
  0.8 0.9 %copy-start.1 = (s32[64,256]{1,0:T(8,128)S(1)}, s32[64,256]{1,0:T(8,128)}, u32[]{:S(2)}) copy-start(s32[64,256]{1,0:T(8,128)} %lists_ref.1) | copy-start | bytes 196612
  0.8 0.9 %copy-start.2 = (s32[64,256]{1,0:T(8,128)S(1)}, s32[64,256]{1,0:T(8,128)}, u32[]{:S(2)}) copy-start(s32[64,256]{1,0:T(8,128)} %bins_ref.1) | copy-start | bytes 196612
  0.8 0.9 %copy-start.3 = (s32[64]{0:T(128)S(1)}, s32[64]{0:T(128)}, u32[]{:S(2)}) copy-start(s32[64]{0:T(128)} %counts_ref.1) | copy-start | bytes 772
  0.8 1.0 %copy-start.4 = (s32[64]{0:T(128)S(1)}, s32[64]{0:T(128)}, u32[]{:S(2)}) copy-start(s32[64]{0:T(128)} %groups_ref.1) | copy-start | bytes 772
  1.8 0.9 %copy-start = (f32[64,3,256]{2,0,1:T(8,128)S(1)}, f32[64,3,256]{2,0,1:T(8,128)}, u32[]{:S(2)}) copy-start(f32[64,3,256]{2,0,1:T(8,128)} %param.9) | copy-start | bytes 589828

commit v5 on v4

--- a/solution.py
+++ b/solution.py
@@ -16,8 +16,8 @@
 TOP = 4
 BLK = 64
 NODE_DEV = 4096
-FIRST = 2
-SECOND = 30
+FIRST = 8
+SECOND = 32
 SHARE = GROUPS // N_SUB
 MESH = pl.DeviceIdType.MESH
 F32 = jnp.float32
@@ -79,23 +79,34 @@
         to_sub(src_of(peer), dst, send, recv, peer, me, me).wait_send()
 
 
-def dom_copy(src, dst, send, recv, peer, slot):
+def dom_copy(src, dst, send, recv, me, step):
     return pltpu.make_async_remote_copy(
-        src_ref=src.at[peer],
-        dst_ref=dst.at[slot],
-        send_sem=send.at[peer],
-        recv_sem=recv.at[slot],
-        device_id={"dom": peer},
+        src_ref=src.at[step],
+        dst_ref=dst.at[N_DOM - step],
+        send_sem=send.at[step],
+        recv_sem=recv.at[N_DOM - step],
+        device_id={"dom": lax.rem(me + step, N_DOM)},
         device_id_type=MESH,
     )
 
 
-def each_dom(me, act):
+def dom_wait(src, dst, send, recv, me, step):
+    pltpu.make_async_remote_copy(
+        src_ref=src.at[step],
+        dst_ref=dst.at[step],
+        send_sem=send.at[step],
+        recv_sem=recv.at[step],
+        device_id={"dom": lax.rem(me + step, N_DOM)},
+        device_id_type=MESH,
+    ).wait_recv()
+
+
+def steps(low, high, act):
     def one(i, carry):
-        act(lax.rem(me + i, N_DOM))
+        act(i)
         return carry
 
-    lax.fori_loop(1, N_DOM, one, 0)
+    lax.fori_loop(low, high, one, 0)
 
 
 def ring_of(me):
@@ -173,7 +184,7 @@
         wait(other(slot))
 
 
-def build_lists(lists_ref, counts_ref, first_list, tiles, pieces, put):
+def build_lists(lists_ref, counts_ref, first_list, tiles, pieces, put, midway):
     highs = tiles.shape[0]
     for c in range(4):
         for p, part in enumerate(thirds(tiles[:, c, :].T)):
@@ -198,26 +209,18 @@
         put(l, jnp.concatenate([0.5 * picked[0], 0.5 * picked[1], 0.5 * picked[2], mass], axis=0))
         return carry
 
-    lax.fori_loop(0, SHARE, one_list, 0)
-
-
-def back_copy(src, dst, k, send, recv, peer, slot):
-    return pltpu.make_async_remote_copy(
-        src_ref=src.at[k, peer],
-        dst_ref=dst.at[slot, k],
-        send_sem=send.at[peer],
-        recv_sem=recv.at[slot],
-        device_id={"dom": peer},
-        device_id_type=MESH,
-    )
-
-
-def spread_tables(lists, wide):
+    lax.fori_loop(0, SHARE // 2, one_list, 0)
+    midway()
+    lax.fori_loop(SHARE // 2, SHARE, one_list, 0)
+
+
+def spread_tables(lists, wide, low, high, owner):
     pick = lax.broadcasted_iota(jnp.int32, (8, 256), 0)
     side = jnp.where(lax.broadcasted_iota(jnp.int32, (8, 256), 1) < 128, 2, 5)
     pick = jnp.where((pick >= side) & (pick < side + 3), 1.0, 0.0).astype(BF16)
 
-    def one(o, carry):
+    def one(p, carry):
+        o = owner(p)
         for l in range(SHARE):
             t = lists[o, l]
             rows = [t[0:1], t[1:2]]
@@ -231,7 +234,7 @@
                 wide[o * SHARE + l, 2 + c] = both[:, 128 * c : 128 * (c + 1)]
         return carry
 
-    lax.fori_loop(0, N_SUB, one, 0)
+    lax.fori_loop(low, high, one, 0)
 
 
 def visit_sums(wide, row, rows, held):
@@ -293,12 +296,12 @@
     t_recv,
     b_send,
     b_recv,
+    e_send,
+    e_recv,
     d_send,
     d_recv,
-    low_send,
-    low_recv,
-    high_send,
-    high_recv,
+    r_send,
+    r_recv,
 ):
     me_dom = lax.axis_index("dom")
     me = lax.axis_index("sub")
@@ -312,6 +315,9 @@
 
     def pattern(mask):
         return jnp.where(mask, 1.0, 0.0).astype(BF16)
+
+    def ahead(goal):
+        return jnp.where(goal < 0, -1, jnp.bitwise_and(goal + (N_DOM - me_dom), N_DOM - 1))
 
     def count(value, matrix):
         return jnp.dot(value.astype(BF16), matrix, preferred_element_type=F32)
@@ -339,7 +345,6 @@
     pl.semaphore_wait(barrier, N_SUB - 1 + N_DOM - 1)
     start_sub(lambda peer: tt_ref, crecv, c_send, c_recv, me)
     ring_one(n_copies)
-    ring_one(p_copies)
     crecv[me] = tt_ref[...]
     nrecv[me] = nodes_ref[...]
     precv[me] = pos_ref[...]
@@ -349,7 +354,8 @@
     marks = [jnp.zeros((N_DOM, 128), F32) for _ in range(2)]
     for pair in range(N_SUB // 2):
         goal = jnp.where(lanes[0:8] < BLK, crecv[2 * pair], crecv[2 * pair + 1])
-        wants = [dom_ids == goal[j : j + 1, :] for j in range(TOP)]
+        steps_to = ahead(goal)
+        wants = [dom_ids == steps_to[j : j + 1, :] for j in range(TOP)]
         ones_of = [jnp.where(w, 1.0, 0.0) for w in wants]
         stack = jnp.concatenate(ones_of, axis=0)
         within, block_total = count(stack, earlier), count(stack, block)
@@ -375,12 +381,14 @@
         codes[2 * pair] = count(kinds, evens)
         codes[2 * pair + 1] = count(kinds, odds)
     ring_two(n_copies, n_wait, ring)
+    ring_one(p_copies)
     own_pair = me // 2
     goal = jnp.where(lanes[0:8] < BLK, crecv[2 * own_pair], crecv[2 * own_pair + 1])
+    steps_to = ahead(goal)
     for t in range(N_SUB):
         hot = jnp.zeros((N_DOM, 128), F32)
         for j in range(TOP):
-            mine = (dom_ids == goal[j : j + 1, :]) & (
+            mine = (dom_ids == steps_to[j : j + 1, :]) & (
                 jnp.bitwise_and(places[own_pair, j], N_SUB - 1) == t
             )
             hot = jnp.where(mine, 1.0, hot)
@@ -388,7 +396,6 @@
     for k in range(2):
         mid[:, k, 6, :] = count(marks[k], full)
         mid[:, k, 7, :] = jnp.zeros((N_DOM, 128), F32)
-    ring_two(p_copies, p_wait, ring)
 
     ring_three(n_copies, n_wait, ring)
     ring_end(n_wait, ring)
@@ -403,8 +410,17 @@
     def put(l, value):
         trecv[me, l] = value
 
-    build_lists(lists_ref, counts_ref, me * SHARE, tiles, pieces, put)
+    build_lists(
+        lists_ref,
+        counts_ref,
+        me * SHARE,
+        tiles,
+        pieces,
+        put,
+        lambda: ring_two(p_copies, p_wait, ring),
+    )
     start_sub(lambda peer: trecv.at[me], trecv, t_send, t_recv, me)
+    spread_tables(trecv, wide, 0, 1, lambda p: me + p)
     ring_three(p_copies, p_wait, ring)
     ring_end(p_wait, ring)
 
@@ -417,12 +433,16 @@
         for k in range(2):
             for h in range(2):
                 mid[:, k, 2 * c + h, :] = rows[N_DOM * k : N_DOM * (k + 1), 128 * h : 128 * (h + 1)]
-    each_dom(me_dom, lambda peer: dom_copy(mid, arr, d_send, d_recv, peer, me_dom).start())
-    arr[me_dom] = jnp.zeros((2, 8, 128), F32)
-    ret[me_dom] = jnp.zeros((2, 8, 128), F32)
-
-    wait_sub_recv(lambda peer: trecv.at[me], trecv, t_send, t_recv, me)
-    spread_tables(trecv, wide)
+    steps(1, N_DOM, lambda i: dom_copy(mid, arr, d_send, d_recv, me_dom, i).start())
+    arr[0] = jnp.zeros((2, 8, 128), F32)
+    ret[0] = jnp.zeros((2, 8, 128), F32)
+
+    def arrived(p):
+        peer = lax.rem(me + p, N_SUB)
+        to_sub(trecv.at[me], trecv, t_send, t_recv, peer, peer, me).wait_recv()
+        return peer
+
+    spread_tables(trecv, wide, 1, N_SUB, arrived)
 
     def home_rows(v):
         rows = [pos_ref[c, pl.ds(v, 1), :] for c in range(3)]
@@ -443,7 +463,7 @@
         home_flush(high - 1)
 
     home_blocks(0, FIRST)
-    each_dom(me_dom, lambda peer: dom_copy(mid, arr, d_send, d_recv, peer, peer).wait_recv())
+    steps(1, N_DOM, lambda i: dom_wait(mid, arr, d_send, d_recv, me_dom, i))
     diagonal = dom_ids == lax.broadcasted_iota(jnp.int32, (N_DOM, 128), 1)
     marks = [
         jnp.sum(jnp.where(diagonal, arr[:, k, 6, :], 0.0), axis=0, keepdims=True) for k in range(2)
@@ -454,42 +474,63 @@
     to_scalars.start()
     to_scalars.wait()
 
-    def imports(k, send, recv):
-        def flush(i):
+    def imports(low, high):
+        def flush(n):
             rows = [jnp.sum(held[q], axis=0, keepdims=True) for q in range(6)]
             rows.append(jnp.zeros((2, 128), F32))
-            pulls[k, lax.rem(me_dom + i, N_DOM)] = jnp.concatenate(rows, axis=0)
-
-        def one(i, carry):
-            flush(jnp.maximum(i - 1, 1))
-            peer = lax.rem(me_dom + i, N_DOM)
-            row = rows_ref[k, peer]
-            visit_sums(wide, row, [arr[peer, k, q : q + 1, :] for q in range(6)], held)
+            pulls[n // 2, lax.rem(n, 2)] = jnp.concatenate(rows, axis=0)
+
+        def one(n, carry):
+            flush(jnp.maximum(n - 1, 2 * low))
+            i, k = n // 2, lax.rem(n, 2)
+            visit_sums(wide, rows_ref[k, i], [arr[i, k, q : q + 1, :] for q in range(6)], held)
             return carry
 
-        lax.fori_loop(1, N_DOM, one, 0)
-        flush(N_DOM - 1)
-        each_dom(me_dom, lambda peer: back_copy(pulls, ret, k, send, recv, peer, me_dom).start())
-
-    imports(0, low_send, low_recv)
-    imports(1, high_send, high_recv)
-
+        lax.fori_loop(2 * low, 2 * high, one, 0)
+        flush(2 * high - 1)
+        steps(low, high, lambda i: dom_copy(pulls, ret, r_send, r_recv, me_dom, i).start())
+
+    def hand_back(low, send, recv):
+        rows = pl.ds(low, N_DOM // 2)
+        steps(max(low, 1), low + N_DOM // 2, lambda i: dom_wait(pulls, ret, r_send, r_recv, me_dom, i))
+        for q in range(6):
+            first, second = ret[rows, 0, q, :], ret[rows, 1, q, :]
+            for t in range(N_SUB):
+                code = codes[t, rows, :]
+                value = jnp.where(code > 1.5, second, jnp.where(code > 0.5, first, 0.0))
+                bsend[t, rows, 128 * q : 128 * (q + 1)] = value
+        back_part(low, send, recv, True)
+        brecv[me, rows] = bsend[me, rows]
+
+    def back_part(low, send, recv, start):
+        rows = pl.ds(low, N_DOM // 2)
+        for p in range(1, N_SUB):
+            peer = lax.rem(me + p, N_SUB)
+            copy = pltpu.make_async_remote_copy(
+                src_ref=bsend.at[peer, rows],
+                dst_ref=brecv.at[me if start else peer, rows],
+                send_sem=send.at[peer],
+                recv_sem=recv.at[me if start else peer],
+                device_id={"sub": peer},
+                device_id_type=MESH,
+            )
+            if start:
+                copy.start()
+            else:
+                copy.wait_recv()
+                copy.wait_send()
+
+    half = N_DOM // 2
+    imports(half + 1, N_DOM)
+    imports(1, half + 1)
+    hand_back(0, b_send, b_recv)
     home_blocks(FIRST, SECOND)
-
-    for k, send, recv in ((0, low_send, low_recv), (1, high_send, high_recv)):
-        each_dom(me_dom, lambda peer: back_copy(pulls, ret, k, send, recv, peer, peer).wait_recv())
-    for q in range(6):
-        low, high = ret[:, 0, q, :], ret[:, 1, q, :]
-        for t in range(N_SUB):
-            code = codes[t]
-            value = jnp.where(code > 1.5, high, jnp.where(code > 0.5, low, 0.0))
-            bsend[t, :, 128 * q : 128 * (q + 1)] = value
-    start_sub(lambda peer: bsend.at[peer], brecv, b_send, b_recv, me)
-    brecv[me] = bsend[me]
+    hand_back(half, e_send, e_recv)
 
     home_blocks(SECOND, BLK)
 
-    wait_sub_recv(lambda peer: bsend.at[peer], brecv, b_send, b_recv, me)
+    back_part(0, b_send, b_recv, False)
+    back_part(half, e_send, e_recv, False)
     active = jnp.where(bins_ref[...] <= CUR_BIN, 1.0, 0.0)
     picks = hots[...]
     for c in range(3):
@@ -506,10 +547,8 @@
     for copy in n_copies + p_copies:
         copy.wait_send()
     wait_sub_send(lambda peer: trecv.at[me], trecv, t_send, t_recv, me)
-    wait_sub_send(lambda peer: bsend.at[peer], brecv, b_send, b_recv, me)
-    each_dom(me_dom, lambda peer: dom_copy(mid, arr, d_send, d_recv, peer, me_dom).wait_send())
-    for k, send, recv in ((0, low_send, low_recv), (1, high_send, high_recv)):
-        each_dom(me_dom, lambda peer: back_copy(pulls, ret, k, send, recv, peer, me_dom).wait_send())
+    steps(1, N_DOM, lambda i: dom_copy(mid, arr, d_send, d_recv, me_dom, i).wait_send())
+    steps(1, N_DOM, lambda i: dom_copy(pulls, ret, r_send, r_recv, me_dom, i).wait_send())
 
 
 def whole(counts, groups, tt, pos, nodes, lists, bins):
@@ -537,7 +576,7 @@
             pltpu.VMEM((GROUPS, 4, LIST, 128), F32),
             pltpu.VMEM((6, 8, 128), F32),
             pltpu.VMEM((3, BLK, 256), F32),
-            pltpu.VMEM((2, N_DOM, 8, 128), F32),
+            pltpu.VMEM((N_DOM, 2, 8, 128), F32),
             pltpu.VMEM((N_DOM, 2, 8, 128), F32),
             pltpu.VMEM((N_SUB, N_DOM, 768), F32),
             pltpu.VMEM((N_SUB, N_DOM, 768), F32),
@@ -548,8 +587,8 @@
         + [dma((N_SUB,)), dma((N_SUB + 2,))]
         + [dma((N_SUB,))] * 2
         + [dma((N_SUB,)), dma((N_SUB + 2,))]
-        + [dma((N_SUB,))] * 4
-        + [dma((N_DOM,))] * 6,
+        + [dma((N_SUB,))] * 6
+        + [dma((N_DOM,))] * 4,
         compiler_params=pltpu.CompilerParams(
             collective_id=0, has_side_effects=True, vmem_limit_bytes=50 * 2**20
         ),

time: 85.5 us -> 79.8 us (0.933)
  Pallas kernels: 81.9 us -> 76.2 us
    pallas_call x1, Pallas kernels: 81.9 us -> 76.2 us  [whole(): pl.pallas_call(whole_kernel, out_shape=jax.ShapeDtypeStruct((3, BLK, 256)...]
where the time goes in v5:
time: 79.8 us; the launch traced here: 79.6 us
  Pallas kernels  76.2 us (95%)
  other arithmetic  1.7 us (2%)
  local copies, waits for them, and re-layouts  1.62 us (2%)
    pallas_call x1, Pallas kernels, whole(): pl.pallas_call(whole_kernel, out_shape=jax.ShapeDtypeStruct((3, BLK, 256)...  76.2 us
    unnamed x13, local copies, waits for them, and re-layouts  1.62 us

profile of v5, /device:TPU:1, one launch (start us, length us, event | category | flops | bytes accessed | tf_op | source)
XLA Modules:
  0.0 79.6 jit_solution(11665980566044424120)
XLA Ops:
  0.0 0.0 copy-start.5
  0.0 0.7 add_bitcast_fusion
  0.7 0.1 pad_add_fusion.tt_ref
  0.8 0.0 copy-done.5
  0.8 0.0 copy-start.1
  0.8 0.0 copy-start.2
  0.8 0.0 copy-start.3
  0.8 0.0 copy-start.4
  0.8 0.9 %pad_maximum_fusion.nodes_ref = f32[4,4096]{1,0:T(4,128)S(1)} fusion(f32[1,4096]{1,0:T(1,128)S(1)} %bitcast.7, f32[3,4096]{1,0:T(4,128)} %param.14), kind=kLoop, calls=%fused_computation | loop fusion | flops 16384 | bytes 131072 | tf_op jit(solution)/shard_map/concatenate | solution.py:611
  1.7 0.0 copy-done.1
  1.7 0.0 copy-done.2
  1.8 0.0 copy-done.3
  1.8 0.0 copy-done.4
  1.8 0.0 copy-start
  1.8 0.9 %copy-done = f32[64,3,256]{2,0,1:T(8,128)S(1)} copy-done((f32[64,3,256]{2,0,1:T(8,128)S(1)}, f32[64,3,256]{2,0,1:T(8,128)}, u32[]{:S(2)}) %copy-start) | copy-done | bytes 196632
  2.7 76.2 %shard_map.91 = f32[3,64,256]{2,1,0:T(8,128)S(1)} custom-call(s32[64]{0:T(128)S(1)} %copy-done.3, s32[64]{0:T(128)S(1)} %copy-done.4, s32[8,128]{1,0:T(8,128)S(1)} %pad_add_fusion.tt_ref, f32[3,64,256]{2,1,0:T(8,128)S(1)} %bitcast.6, f32[4,4096]{1,0:T(4,128)S(1)} %pad_maximum_fusion.nodes_ref, s32[64,256]{1,0:T(8,128)S(1)} %copy-done.1, s32[64,256]{1,0:T(8,128)S(1)} %copy-done.2), custom_call_target="tpu_custom_call" | custom-call | tf_op jit(solution)/shard_map/pallas_call | solution.py:558
  78.9 0.7 copy.11
Async XLA Ops:
  0.0 0.8 %copy-start.5 = (f32[4096]{0:T(1024)S(1)}, f32[4096]{0:T(1024)}, u32[]{:S(2)}) copy-start(f32[4096]{0:T(1024)} %param.15) | copy-start | bytes 49156
  0.8 0.9 %copy-start.1 = (s32[64,256]{1,0:T(8,128)S(1)}, s32[64,256]{1,0:T(8,128)}, u32[]{:S(2)}) copy-start(s32[64,256]{1,0:T(8,128)} %lists_ref.1) | copy-start | bytes 196612
  0.8 0.9 %copy-start.2 = (s32[64,256]{1,0:T(8,128)S(1)}, s32[64,256]{1,0:T(8,128)}, u32[]{:S(2)}) copy-start(s32[64,256]{1,0:T(8,128)} %bins_ref.1) | copy-start | bytes 196612
  0.8 0.9 %copy-start.3 = (s32[64]{0:T(128)S(1)}, s32[64]{0:T(128)}, u32[]{:S(2)}) copy-start(s32[64]{0:T(128)} %counts_ref.1) | copy-start | bytes 772
  0.8 1.0 %copy-start.4 = (s32[64]{0:T(128)S(1)}, s32[64]{0:T(128)}, u32[]{:S(2)}) copy-start(s32[64]{0:T(128)} %groups_ref.1) | copy-start | bytes 772
  1.8 0.9 %copy-start = (f32[64,3,256]{2,0,1:T(8,128)S(1)}, f32[64,3,256]{2,0,1:T(8,128)}, u32[]{:S(2)}) copy-start(f32[64,3,256]{2,0,1:T(8,128)} %param.9) | copy-start | bytes 589828

commit v6 on v5

--- a/solution.py
+++ b/solution.py
@@ -16,8 +16,8 @@
 TOP = 4
 BLK = 64
 NODE_DEV = 4096
-FIRST = 8
-SECOND = 32
+FIRST = 14
+SECOND = 38
 SHARE = GROUPS // N_SUB
 MESH = pl.DeviceIdType.MESH
 F32 = jnp.float32

time: 79.8 us -> 80.3 us (level)
  no operation moved by 1% of the time
where the time goes in v6:
time: 80.3 us; the launch traced here: 80.1 us
  Pallas kernels  76.7 us (96%)
  other arithmetic  1.7 us (2%)
  local copies, waits for them, and re-layouts  1.62 us (2%)
    pallas_call x1, Pallas kernels, whole(): pl.pallas_call(whole_kernel, out_shape=jax.ShapeDtypeStruct((3, BLK, 256)...  76.7 us
    unnamed x13, local copies, waits for them, and re-layouts  1.62 us

profile of v6, /device:TPU:1, one launch (start us, length us, event | category | flops | bytes accessed | tf_op | source)
XLA Modules:
  0.0 80.1 jit_solution(14468895080663584740)
XLA Ops:
  0.0 0.0 copy-start.5
  0.0 0.7 add_bitcast_fusion
  0.7 0.1 pad_add_fusion.tt_ref
  0.8 0.0 copy-done.5
  0.8 0.0 copy-start.1
  0.8 0.0 copy-start.2
  0.8 0.0 copy-start.3
  0.8 0.0 copy-start.4
  0.8 0.9 %pad_maximum_fusion.nodes_ref = f32[4,4096]{1,0:T(4,128)S(1)} fusion(f32[1,4096]{1,0:T(1,128)S(1)} %bitcast.7, f32[3,4096]{1,0:T(4,128)} %param.14), kind=kLoop, calls=%fused_computation | loop fusion | flops 16384 | bytes 131072 | tf_op jit(solution)/shard_map/concatenate | solution.py:611
  1.7 0.0 copy-done.1
  1.7 0.0 copy-done.2
  1.8 0.0 copy-done.3
  1.8 0.0 copy-done.4
  1.8 0.0 copy-start
  1.8 0.9 %copy-done = f32[64,3,256]{2,0,1:T(8,128)S(1)} copy-done((f32[64,3,256]{2,0,1:T(8,128)S(1)}, f32[64,3,256]{2,0,1:T(8,128)}, u32[]{:S(2)}) %copy-start) | copy-done | bytes 196632
  2.7 76.7 %shard_map.91 = f32[3,64,256]{2,1,0:T(8,128)S(1)} custom-call(s32[64]{0:T(128)S(1)} %copy-done.3, s32[64]{0:T(128)S(1)} %copy-done.4, s32[8,128]{1,0:T(8,128)S(1)} %pad_add_fusion.tt_ref, f32[3,64,256]{2,1,0:T(8,128)S(1)} %bitcast.6, f32[4,4096]{1,0:T(4,128)S(1)} %pad_maximum_fusion.nodes_ref, s32[64,256]{1,0:T(8,128)S(1)} %copy-done.1, s32[64,256]{1,0:T(8,128)S(1)} %copy-done.2), custom_call_target="tpu_custom_call" | custom-call | tf_op jit(solution)/shard_map/pallas_call | solution.py:558
  79.4 0.7 copy.11
Async XLA Ops:
  0.0 0.8 copy-start.5
  0.8 0.9 %copy-start.1 = (s32[64,256]{1,0:T(8,128)S(1)}, s32[64,256]{1,0:T(8,128)}, u32[]{:S(2)}) copy-start(s32[64,256]{1,0:T(8,128)} %lists_ref.1) | copy-start | bytes 196612
  0.8 0.9 %copy-start.2 = (s32[64,256]{1,0:T(8,128)S(1)}, s32[64,256]{1,0:T(8,128)}, u32[]{:S(2)}) copy-start(s32[64,256]{1,0:T(8,128)} %bins_ref.1) | copy-start | bytes 196612
  0.8 0.9 %copy-start.3 = (s32[64]{0:T(128)S(1)}, s32[64]{0:T(128)}, u32[]{:S(2)}) copy-start(s32[64]{0:T(128)} %counts_ref.1) | copy-start | bytes 772
  0.8 1.0 %copy-start.4 = (s32[64]{0:T(128)S(1)}, s32[64]{0:T(128)}, u32[]{:S(2)}) copy-start(s32[64]{0:T(128)} %groups_ref.1) | copy-start | bytes 772
  1.8 0.9 %copy-start = (f32[64,3,256]{2,0,1:T(8,128)S(1)}, f32[64,3,256]{2,0,1:T(8,128)}, u32[]{:S(2)}) copy-start(f32[64,3,256]{2,0,1:T(8,128)} %param.9) | copy-start | bytes 589828
